TPU v7x, 32 devices: a whole 2x2x4 slice. The times are simulated.
32 devices in a mesh: replica: 8 (over z, y), tensor: 4 (over x, core).
Axes of the slice: x: 2, y: 2, z: 4, core: 2. Of those that a mesh axis runs over, the one named last changes fastest.
Arguments:
- base_stream: bfloat16 [32, 8192], P('tensor', 'replica'), may hold values from -6 to 6
- out_weight: bfloat16 [64, 128, 8192], P('tensor', 'replica'), may hold values from -0.5 to 0.5
- queries: bfloat16 [4, 32, 64, 128], P(None, 'replica', 'tensor'), may hold values from -5 to 5
- cache_keys: bfloat16 [32, 8, 1536, 128], P('replica', 'tensor'), may hold values from -5 to 5
- cache_values: bfloat16 [32, 8, 1536, 128], P('replica', 'tensor'), may hold values from -6 to 6
- new_keys: bfloat16 [4, 32, 8, 128], P(None, 'replica', 'tensor'), may hold values from -5 to 5
- new_values: bfloat16 [4, 32, 8, 128], P(None, 'replica', 'tensor'), may hold values from -6 to 6
- lengths: int32 [32], P('replica'), may hold values from 384 to 1536
- finished: int32 [32], replicated, may hold values 0 or 1
- owners: int32 [32, 1], replicated, may hold values from 0 to 7; in each aligned block of 32 rows (0 to 31, 32 to 63, ...) at most 4 rows name the same one
Outputs:
- updates: bfloat16 [4, 32, 8192], P(None, 'tensor', 'replica')
- trainer_rows: bfloat16 [8, 4, 8192], P('replica', 'tensor')
Inputs may be any that keep to these rules, and one draw needn't show every extreme that they name: `owners`: no owner is named by more than 4 rows, and one owner is named by exactly 4.
All inputs are finite; a program needn't handle non-finite values.
Results may differ from a plain program's by a relative error of at most 0.013.
Values may be sent and summed in bfloat16 or wider, within the bound.
No kernel may reach another device: no remote copies, remote signals or barrier semaphores. Data moves between devices by JAX's collectives and lax.ppermute only.
A program may use at most 128 MiB of HBM per device.

v0:
```python
import math

import jax
import jax.numpy as jnp
from jax import lax
from jax.sharding import PartitionSpec as P

SLOT_DEV = 1


def attend(queries, cache_keys, cache_values, new_keys, new_values, lengths):
    steps_count, row_count, heads_here, head_size = queries.shape
    kv_here = cache_keys.shape[1]
    positions_count = cache_keys.shape[2]
    group_size = heads_here // kv_here
    score_scale = 1.0 / math.sqrt(head_size)
    grouped = queries.reshape(steps_count, row_count, kv_here, group_size, head_size)
    cache_scores = (
        jnp.einsum("tbgqd,bgcd->tbgqc", grouped, cache_keys, preferred_element_type=jnp.float32)
        * score_scale
    )
    positions = lax.broadcasted_iota(jnp.int32, (1, row_count, 1, 1, positions_count), 4)
    is_valid = positions < lengths[None, :, None, None, None]
    cache_scores = jnp.where(is_valid, cache_scores, jnp.float32(-1e30))
    fresh_scores = (
        jnp.einsum("tbgqd,ubgd->tbgqu", grouped, new_keys, preferred_element_type=jnp.float32)
        * score_scale
    )
    step_now = lax.broadcasted_iota(jnp.int32, (steps_count, 1, 1, 1, steps_count), 0)
    step_then = lax.broadcasted_iota(jnp.int32, (steps_count, 1, 1, 1, steps_count), 4)
    fresh_scores = jnp.where(step_then <= step_now, fresh_scores, jnp.float32(-1e30))
    highest = jnp.maximum(
        jnp.max(cache_scores, axis=-1, keepdims=True), jnp.max(fresh_scores, axis=-1, keepdims=True)
    )
    cache_weights = jnp.exp(cache_scores - highest)
    fresh_weights = jnp.exp(fresh_scores - highest)
    totals = jnp.sum(cache_weights, axis=-1, keepdims=True) + jnp.sum(
        fresh_weights, axis=-1, keepdims=True
    )
    cache_probs = (cache_weights / totals).astype(jnp.bfloat16)
    fresh_probs = (fresh_weights / totals).astype(jnp.bfloat16)
    mixed = jnp.einsum(
        "tbgqc,bgcd->tbgqd", cache_probs, cache_values, preferred_element_type=jnp.float32
    )
    mixed = mixed + jnp.einsum(
        "tbgqu,ubgd->tbgqd", fresh_probs, new_values, preferred_element_type=jnp.float32
    )
    return mixed.reshape(steps_count, row_count, heads_here * head_size).astype(jnp.bfloat16)


def reduce_heads(partial_value):
    rounded = partial_value.astype(jnp.bfloat16)
    totals = lax.psum(rounded, "tensor").astype(jnp.float32)
    share = totals.shape[1] // lax.axis_size("tensor")
    return lax.dynamic_slice_in_dim(totals, lax.axis_index("tensor") * share, share, 1)


def shards(
    base_stream,
    out_weight,
    queries,
    cache_keys,
    cache_values,
    new_keys,
    new_values,
    lengths,
    finished,
    owners,
):
    heads_here = out_weight.shape[0]
    regrouped = lax.all_to_all(out_weight, "replica", split_axis=2, concat_axis=1, tiled=True)
    weight_local = regrouped.reshape(heads_here * regrouped.shape[1], regrouped.shape[2])
    attended = attend(queries, cache_keys, cache_values, new_keys, new_values, lengths)
    partial_value = jnp.einsum(
        "tbf,fc->tbc",
        lax.all_gather(attended, "replica", axis=1, tiled=True),
        weight_local,
        preferred_element_type=jnp.float32,
    )
    summed = reduce_heads(partial_value)
    updates = summed.astype(jnp.bfloat16)
    stream = base_stream.astype(jnp.float32) + jnp.sum(updates.astype(jnp.float32), axis=0)
    stream_rounded = stream.astype(jnp.bfloat16)
    all_streams = lax.all_gather(stream_rounded, "tensor", axis=0, tiled=True)
    owner_count = lax.axis_size("replica")
    owner_ids = lax.broadcasted_iota(jnp.int32, (1, owner_count), 1)
    onehot = (owners == owner_ids).astype(jnp.int32)
    before = jnp.cumsum(onehot, axis=0) - onehot
    slot_rank = jnp.sum(before * onehot, axis=1)
    first_slot = lax.axis_index("tensor") * SLOT_DEV
    slot_ids = first_slot + lax.broadcasted_iota(jnp.int32, (1, 1, SLOT_DEV), 2)
    chosen = (
        onehot[:, :, None]
        * (slot_rank[:, None, None] == slot_ids).astype(jnp.int32)
        * finished[:, None, None]
    )
    selector = chosen.astype(jnp.bfloat16)
    outgoing = jnp.einsum(
        "jos,jc->osc", selector, all_streams, preferred_element_type=jnp.float32
    ).astype(jnp.bfloat16)
    trainer_rows = lax.all_to_all(outgoing, "replica", split_axis=0, concat_axis=2, tiled=True)
    return (updates, trainer_rows)


def solution(mesh):
    placed = (
        P("tensor", "replica"),
        P("tensor", "replica", None),
        P(None, "replica", "tensor", None),
        P("replica", "tensor", None, None),
        P("replica", "tensor", None, None),
        P(None, "replica", "tensor", None),
        P(None, "replica", "tensor", None),
        P("replica"),
        P(),
        P(),
    )
    return jax.shard_map(
        shards,
        mesh=mesh,
        in_specs=placed,
        out_specs=(P(None, "tensor", "replica"), P("replica", "tensor", None)),
        check_vma=False,
    )
```

profile of v0, /device:TPU:0, one launch (start us, length us, event | category | flops | bytes accessed | tf_op | source)
XLA Modules:
  0.0 318.9 jit_solution(999825138677871653)
XLA Ops:
  7.2 0.0 copy-start
  7.2 27.8 %copy.29 = bf16[16,16,8192]{1,0,2:T(8,128)(2,1)} copy(bf16[16,16,8192]{2,1,0:T(8,128)(2,1)} %param.11) | data formatting | bytes 8388608 | tf_op args[1]
  35.0 37.7 %reshape.116 = bf16[8,2,131072]{2,1,0:T(2,128)(2,1)} reshape(bf16[8192,16,16]{2,1,0:T(8,128)(2,1)} %bitcast.60) | data formatting | bytes 8388608
  72.7 0.0 copy-start.2
  72.7 0.0 copy-start.7
  72.7 0.0 copy-start.5
  72.7 7.4 %all-to-all-start = ((bf16[8,2,131072]{2,1,0:T(2,128)(2,1)}), bf16[8,2,131072]{2,1,0:T(2,128)(2,1)}, u32[]{:S(2)}, u32[]{:S(2)}) async-start(bf16[8,2,131072]{2,1,0:T(2,128)(2,1)} %reshape.116), calls=%async_computation | async-start | bytes 8388608 | tf_op jit(solution)/shard_map/all_to_all | solution.py:71
  80.2 0.0 all-reduce.2.cloned.1.call-start
  80.2 0.0 copy-done.2
  80.2 0.0 copy-done.7
  80.2 0.4 fusion.44
  80.7 0.0 copy-done.5
  80.7 0.1 iota_compare_fusion
  80.8 0.0 copy-done
  80.8 0.0 copy-start.8
  80.8 0.0 copy-start.6
  80.8 1.2 fusion.43
  82.0 0.1 fusion.31
  82.1 0.4 fusion.13
  82.5 0.0 copy-done.8
  82.5 0.2 fusion.32
  82.7 0.0 copy-done.6
  82.7 0.0 copy-start.4
  82.7 0.7 fusion.20
  83.5 0.0 copy-done.4
  83.5 0.1 fusion.35
  83.6 0.1 reduce_window_sum.11
  83.6 0.2 select_reduce_fusion
  83.8 112.7 %all_gather.6 = bf16[4,32,2048]{2,0,1:T(4,128)(2,1)} all-gather(bf16[4,4,2048]{2,0,1:T(4,128)(2,1)S(1)} %reshape.115), channel_id=1, replica_groups=mesh['replica'=8,'tensor'=4] {'replica'}, dimensions={1}, use_global_device_ids=true | all-gather | bytes 589824 | tf_op jit(solution)/shard_map/all_gather | solution.py:76
  196.5 0.0 all-to-all-done
  196.5 25.8 %reshape.117 = bf16[8192,16,16]{2,1,0:T(8,128)(2,1)} reshape(bf16[8,2,131072]{2,1,0:T(2,128)(2,1)} %all-to-all-done) | data formatting | bytes 8388608
  222.3 32.9 %copy.30 = bf16[16,16,8,1024]{3,1,2,0:T(8,128)(2,1)} copy(bf16[16,16,8,1024]{1,0,3,2:T(8,128)(2,1)} %bitcast.59) | data formatting | bytes 8388608 | tf_op jit(solution)/shard_map/all_to_all | solution.py:71
  255.2 0.0 copy-start.1
  255.2 0.0 copy-start.3
  255.2 0.0 copy-start.9
  255.2 4.2 %convolution_convert_fusion = bf16[4,32,1024]{2,1,0:T(8,128)(2,1)} fusion(bf16[2048,1024,1]{1,0,2:T(8,128)(2,1)} %bitcast.61, bf16[4,32,2048]{2,0,1:T(4,128)(2,1)} %all_gather.6), kind=kOutput, calls=%fused_computation.10 | convolution fusion | flops 537001984 | bytes 4980736 | tf_op jit(solution)/shard_map/tbf,fc->tbc/dot_general | solution.py:74
  259.4 0.0 all-reduce.2.cloned.1.call-update
  259.5 31.9 %all-reduce.2.cloned.1.call-done = bf16[4,32,1024]{2,1,0:T(8,128)(2,1)} async-done(((bf16[4,32,1024]{2,1,0:T(8,128)(2,1)}), bf16[4,32,1024]{2,1,0:T(8,128)(2,1)}) %all-reduce.2.cloned.1.call-update) | async-done | bytes 262160 | tf_op jit(solution)/shard_map/psum | solution.py:53
  291.3 1.5 convert_reduce_fusion
  292.8 0.0 copy-done.3
  292.8 5.2 %all_gather.7 = bf16[32,1024]{1,0:T(8,128)(2,1)S(1)} all-gather(bf16[8,1024]{1,0:T(8,128)(2,1)S(1)} %add_convert_fusion), channel_id=1, replica_groups=mesh['replica'=8,'tensor'=4] {'tensor'}, dimensions={0}, use_global_device_ids=true | all-gather | bytes 81920 | tf_op jit(solution)/shard_map/all_gather | solution.py:84
  298.1 0.0 copy-done.9
  298.1 0.3 fusion.25
  298.3 0.5 broadcast.58
  298.9 0.7 reduce
  299.5 11.9 %all_to_all.27 = bf16[8,2,512]{2,1,0:T(2,128)(2,1)S(1)} all-to-all(bf16[8,2,512]{2,1,0:T(2,128)(2,1)S(1)} %reshape.118), channel_id=1, replica_groups=mesh['replica'=8,'tensor'=4] {'replica'}, dimensions={0} | all-to-all | bytes 32768 | tf_op jit(solution)/shard_map/all_to_all | solution.py:101
  311.4 0.6 reshape.119
  312.1 0.0 copy-done.1
  (8 shorter events, 0.1 us)
Async XLA Ops:
  7.2 73.6 %copy-start = (bf16[4,2,1536,128]{3,2,1,0:T(8,128)(2,1)S(1)}, bf16[4,2,1536,128]{3,2,1,0:T(8,128)(2,1)}, u32[]{:S(2)}) copy-start(bf16[4,2,1536,128]{3,2,1,0:T(8,128)(2,1)} %param.13) | copy-start | bytes 9437188
  72.7 7.5 %copy-start.2 = (bf16[4,4,16,128]{3,2,1,0:T(8,128)(2,1)S(1)}, bf16[4,4,16,128]{3,2,1,0:T(8,128)(2,1)}, u32[]{:S(2)}) copy-start(bf16[4,4,16,128]{3,2,1,0:T(8,128)(2,1)} %param.12) | copy-start | bytes 196612
  72.7 7.5 %copy-start.7 = (bf16[4,4,2,128]{3,2,1,0:T(2,128)(2,1)S(1)}, bf16[4,4,2,128]{3,2,1,0:T(2,128)(2,1)}, u32[]{:S(2)}) copy-start(bf16[4,4,2,128]{3,2,1,0:T(2,128)(2,1)} %param.15) | copy-start | bytes 24580
  72.7 8.0 %copy-start.5 = (s32[4]{0:T(128)S(1)}, s32[4]{0:T(128)}, u32[]{:S(2)}) copy-start(s32[4]{0:T(128)} %param.17) | copy-start | bytes 52
  72.7 123.8 %all-to-all-start = ((bf16[8,2,131072]{2,1,0:T(2,128)(2,1)}), bf16[8,2,131072]{2,1,0:T(2,128)(2,1)}, u32[]{:S(2)}, u32[]{:S(2)}) async-start(bf16[8,2,131072]{2,1,0:T(2,128)(2,1)} %reshape.116), calls=%async_computation | async-start | bytes 8388608 | tf_op jit(solution)/shard_map/all_to_all | solution.py:71
  80.2 211.2 %all-reduce.2.cloned.1.call-start = ((), (), s32[]{:S(2)}) async-start(), calls=%async_computation.2 | async-start | bytes 524288 | tf_op jit(solution)/shard_map/psum | solution.py:53
  80.8 1.7 copy-start.8
  80.8 1.9 copy-start.6
  82.7 0.8 copy-start.4
  255.2 56.9 %copy-start.1 = (bf16[4,2,1536,128]{3,2,1,0:T(8,128)(2,1)S(1)}, bf16[4,2,1536,128]{3,2,1,0:T(8,128)(2,1)}, u32[]{:S(2)}) copy-start(bf16[4,2,1536,128]{3,2,1,0:T(8,128)(2,1)} %param.13) | copy-start | bytes 9437188
  255.2 37.6 %copy-start.3 = (bf16[8,1024]{1,0:T(8,128)(2,1)S(1)}, bf16[8,1024]{1,0:T(8,128)(2,1)}, u32[]{:S(2)}) copy-start(bf16[8,1024]{1,0:T(8,128)(2,1)} %param.10) | copy-start | bytes 49156
  255.2 42.9 %copy-start.9 = (s32[32]{0:T(128)S(1)}, s32[32]{0:T(128)}, u32[]{:S(2)}) copy-start(s32[32]{0:T(128)} %param.18) | copy-start | bytes 388
Sparse Core Ops, SparseCore 0:
  259.6 31.7 all-reduce.1
where the time goes:
time: 321 us; the launch traced here: 319 us
  blocking collectives  130 us (40%)
  local copies, waits for them, and re-layouts  125 us (39%)
  waiting for transfers between devices  31.9 us (10%)
  between operations  14.2 us (4%)
  starting transfers between devices  7.48 us (2%)
  matrix products  7.07 us (2%)
    all_gather x1, blocking collectives, shards(): lax.all_gather(attended, 'replica', axis=1, tiled=True)  113 us
    unnamed x25, local copies, waits for them, and re-layouts  92 us
    all_to_all x1, local copies, waits for them, and re-layouts, shards(): lax.all_to_all(out_weight, 'replica', split_axis=2, concat_axis=1, tiled=...  32.9 us
    psum x1, waiting for transfers between devices, reduce_heads(): totals = lax.psum(rounded, 'tensor').astype(jnp.float32)  31.9 us
    all_to_all x1, blocking collectives, shards(): lax.all_to_all(outgoing, 'replica', split_axis=0, concat_axis=2, tiled=True)  11.9 us
    all_to_all x1, starting transfers between devices, shards(): lax.all_to_all(out_weight, 'replica', split_axis=2, concat_axis=1, tiled=...  7.45 us
  transfers between devices with their start and end apart: 2, of which 1 were waited for; matrix products, arithmetic and copies ran while one was open for 1% of the time, Pallas kernels for 0%

commit v1 on v0

--- a/solution.py
+++ b/solution.py
@@ -1,11 +1,15 @@
+import functools
 import math
 
 import jax
 import jax.numpy as jnp
 from jax import lax
+from jax.experimental import pallas as pl
+from jax.experimental.pallas import tpu as pltpu
 from jax.sharding import PartitionSpec as P
 
 SLOT_DEV = 1
+LANES = 128
 
 
 def attend(queries, cache_keys, cache_values, new_keys, new_values, lengths):
@@ -55,7 +59,7 @@
     return lax.dynamic_slice_in_dim(totals, lax.axis_index("tensor") * share, share, 1)
 
 
-def shards(
+def regroup_weight(
     base_stream,
     out_weight,
     queries,
@@ -102,6 +106,201 @@
     return (updates, trainer_rows)
 
 
+def select_rows(owners, finished, steps_count, row_count, columns):
+    replicas, tensors = lax.axis_size("replica"), lax.axis_size("tensor")
+    me_r, me_t = lax.axis_index("replica"), lax.axis_index("tensor")
+    total_rows = replicas * row_count
+    share = total_rows // tensors
+    width = steps_count * total_rows
+    shape = (tensors, steps_count * share, width)
+    col = lax.broadcasted_iota(jnp.int32, shape, 2)
+    col_row = col // (steps_count * row_count) * row_count + col % row_count
+    col_step = col // row_count % steps_count
+    target = lax.broadcasted_iota(jnp.int32, shape, 0) ^ me_t
+    line = lax.broadcasted_iota(jnp.int32, shape, 1)
+    update_rows = (col_row == target * share + line % share) & (col_step == line // share)
+    names = owners[:, 0]
+    index = jnp.arange(total_rows)
+    rank = jnp.sum((names[None, :] == names[:, None]) & (index[None, :] < index[:, None]), axis=1)
+    spread = lambda v: jnp.broadcast_to(
+        v.reshape(replicas, 1, row_count), (replicas, steps_count, row_count)
+    ).reshape(1, 1, width)
+    shape = (tensors, replicas, width)
+    slot = lax.broadcasted_iota(jnp.int32, shape, 0) ^ me_t
+    owner = lax.broadcasted_iota(jnp.int32, shape, 1) ^ me_r
+    slot_rows = (spread(names) == owner) & (spread(rank) == slot) & (spread(finished) > 0)
+    rows = jnp.concatenate([update_rows, slot_rows], axis=1)
+    own = lax.broadcasted_iota(jnp.int32, (1, 1, share), 2) + me_t * share
+    pick = lambda v: lax.dynamic_slice_in_dim(v, me_t * share, share).reshape(1, 1, share)
+    base_rows = (pick(names) == owner[:, :, :share]) & (pick(rank) == slot[:, :, :share]) & (
+        pick(finished) > 0
+    )
+    return (
+        rows.reshape(-1, width).astype(jnp.bfloat16),
+        base_rows.reshape(-1, share).astype(jnp.bfloat16),
+    )
+
+
+def project_kernel(
+    sizes, me_ref, gathered, rows, base_rows, base, weight, *refs
+):
+    tensors, replicas, lines, slots = sizes
+    outs, (held, slot_sums) = refs[:-2], refs[-2:]
+    step = pl.program_id(0)
+    me = me_ref[0]
+
+    @pl.when(step == 0)
+    def _():
+        held[...] = jnp.dot(
+            rows[...], gathered[...], preferred_element_type=jnp.float32
+        ).astype(jnp.bfloat16)
+
+    block = step ^ me
+    sums = jnp.dot(held[...], weight[...], preferred_element_type=jnp.float32)
+    cols = sums.shape[1]
+    half = cols // 2
+    low, high = step % 2, step // 2
+    for t in range(tensors):
+        first = t * (lines + slots)
+        part = sums[first : first + lines].astype(jnp.bfloat16)
+        a_ref, b_ref = outs[t % 2], outs[2 + t % 2]
+        a_ref[t // 2, low, high, :lines] = part[:, :half]
+        b_ref[low, t // 2, high, :lines] = part[:, half:]
+        for c in range(cols // LANES):
+            slot_sums[t, c, pl.ds(block, slots, stride=replicas), :] = sums[
+                first + lines : first + lines + slots, c * LANES : (c + 1) * LANES
+            ]
+
+    @pl.when(step == 0)
+    def _():
+        extra = jnp.dot(base_rows[...], base[...], preferred_element_type=jnp.float32)
+        for t in range(tensors):
+            for c in range(cols // LANES):
+                slot_sums[t, c, pl.ds(me, slots, stride=replicas), :] += extra[
+                    t * slots : (t + 1) * slots, c * LANES : (c + 1) * LANES
+                ]
+
+    @pl.when(step == pl.num_programs(0) - 1)
+    def _():
+        for t in range(tensors):
+            a_ref, b_ref = outs[t % 2], outs[2 + t % 2]
+            for r in range(replicas):
+                for c in range(cols // LANES):
+                    part = slot_sums[t, c, r * replicas : (r + 1) * replicas].astype(jnp.bfloat16)
+                    at = c * LANES % half
+                    if c * LANES < half:
+                        a_ref[t // 2, r % 2, r // 2, lines:, at : at + LANES] = part
+                    else:
+                        b_ref[r % 2, t // 2, r // 2, lines:, at : at + LANES] = part
+
+
+def project(gathered, rows, base_rows, base_stream, weight):
+    replicas, tensors = lax.axis_size("replica"), lax.axis_size("tensor")
+    depth, model = weight.shape
+    cols = model // replicas
+    slots = replicas
+    lines = rows.shape[0] // tensors - slots
+    me = lax.axis_index("replica").astype(jnp.int32).reshape(1)
+    whole = lambda v: pl.BlockSpec(v.shape, lambda j, me: (0,) * v.ndim)
+    a_shape = (tensors // 2, 2, replicas // 2, lines + replicas, cols // 2)
+    b_shape = (2, tensors // 2, replicas // 2, lines + replicas, cols // 2)
+    shapes = [jax.ShapeDtypeStruct(s, jnp.bfloat16) for s in (a_shape, a_shape, b_shape, b_shape)]
+    return pl.pallas_call(
+        functools.partial(project_kernel, (tensors, replicas, lines, slots)),
+        out_shape=shapes,
+        grid_spec=pltpu.PrefetchScalarGridSpec(
+            num_scalar_prefetch=1,
+            grid=(replicas,),
+            in_specs=[
+                whole(gathered),
+                whole(rows),
+                whole(base_rows),
+                whole(base_stream),
+                pl.BlockSpec((depth, cols), lambda j, me: (0, j ^ me[0])),
+            ],
+            out_specs=[whole(s) for s in shapes],
+            scratch_shapes=[
+                pltpu.VMEM((rows.shape[0], depth), jnp.bfloat16),
+                pltpu.VMEM((tensors, cols // LANES, slots * replicas, LANES), jnp.float32),
+            ],
+        ),
+        cost_estimate=pl.CostEstimate(
+            flops=2 * rows.shape[0] * depth * model,
+            bytes_accessed=2 * depth * model,
+            transcendentals=0,
+        ),
+        name="project",
+    )(me, gathered, rows, base_rows, base_stream, weight)
+
+
+def exchange(value, axis, mask):
+    size = lax.axis_size(axis)
+    return lax.ppermute(value, axis, [(i, i ^ mask) for i in range(size)])
+
+
+def fold(value, axis, bit):
+    came = exchange(value[1].astype(jnp.bfloat16), axis, bit)
+    return value[0] + came.astype(jnp.float32)
+
+
+def move_sums(
+    base_stream,
+    out_weight,
+    queries,
+    cache_keys,
+    cache_values,
+    new_keys,
+    new_values,
+    lengths,
+    finished,
+    owners,
+):
+    steps_count, row_count, heads_here, head_size = queries.shape
+    replicas, tensors = lax.axis_size("replica"), lax.axis_size("tensor")
+    feats = out_weight.shape[1]
+    depth = heads_here * feats
+    model = out_weight.shape[2]
+    cols = model // replicas
+    share = replicas * row_count // tensors
+    lines = steps_count * share
+    attended = attend(queries, cache_keys, cache_values, new_keys, new_values, lengths)
+    split = attended.reshape(steps_count * row_count, heads_here, replicas, feats)
+    split = split.transpose(2, 0, 1, 3).reshape(replicas, steps_count * row_count, depth)
+    gathered = lax.all_to_all(split, "replica", split_axis=0, concat_axis=0, tiled=True)
+    gathered = gathered.reshape(replicas * steps_count * row_count, depth)
+    rows, base_rows = select_rows(owners, finished, steps_count, row_count, cols)
+    weight = out_weight.reshape(depth, model)
+    a_keep, a_send, b_keep, b_send = project(gathered, rows, base_rows, base_stream, weight)
+    f32 = jnp.float32
+    a_sum = a_keep.astype(f32) + exchange(a_send, "tensor", 1).astype(f32)
+    b_sum = b_keep.astype(f32) + exchange(b_send, "tensor", 1).astype(f32)
+    a_sum = fold(a_sum, "tensor", 2)
+    b_sum = fold(b_sum, "replica", 1)
+    a_sum = fold(a_sum, "replica", 1)
+    b_sum = fold(b_sum, "tensor", 2)
+
+    def last(value):
+        total = value[0]
+        for m in range(1, replicas // 2):
+            total = total + exchange(value[m].astype(jnp.bfloat16), "replica", 2 * m).astype(f32)
+        return total.astype(jnp.bfloat16)
+
+    total = jnp.concatenate([last(a_sum), last(b_sum)], axis=1)
+    updates = total[:lines].reshape(steps_count, share, cols)
+    trainer_rows = total[lines:].reshape(1, SLOT_DEV, model)
+    return (updates, trainer_rows)
+
+
+def shards(*arrays):
+    base_stream, out_weight, queries = arrays[:3]
+    steps_count, row_count, heads_here, _ = queries.shape
+    replicas, tensors = lax.axis_size("replica"), lax.axis_size("tensor")
+    sent = steps_count * row_count * replicas
+    few = sent <= heads_here * out_weight.shape[1]
+    paired = tensors == 4 and replicas >= 4 and replicas & (replicas - 1) == 0
+    return (move_sums if few and paired else regroup_weight)(*arrays)
+
+
 def solution(mesh):
     placed = (
         P("tensor", "replica"),

time: 321 us -> 66.7 us (0.21)
  blocking collectives: 130 us -> 0 us
  local copies, waits for them, and re-layouts: 125 us -> 8.39 us
  between operations: 14.2 us -> 0.97 us
  waiting for transfers between devices: 31.9 us -> 20.7 us
  starting transfers between devices: 7.48 us -> 18 us
  Pallas kernels: 0 us -> 7.51 us
  other arithmetic: 3 us -> 6.29 us
    all_gather x2 -> x0, blocking collectives: 118 us -> none  [the longest x1 113 us: shards(): lax.all_gather(attended, 'replica', axis=1, tiled=True)]
    unnamed x25 -> x15, local copies, waits for them, and re-layouts: 92 us -> 1.41 us
    all_to_all x1 -> x0, local copies, waits for them, and re-layouts: 32.9 us -> none  [shards(): lax.all_to_all(out_weight, 'replica', split_axis=2, concat_axis=1, tiled=...]
    psum x1 -> x0, waiting for transfers between devices: 31.9 us -> none  [reduce_heads(): totals = lax.psum(rounded, 'tensor').astype(jnp.float32)]
    ppermute x0 -> x12, waiting for transfers between devices: none -> 17.9 us  [exchange(): return lax.ppermute(value, axis, [(i, i ^ mask) for i in range(size)])]
    all_to_all x1 -> x0, blocking collectives: 11.9 us -> none  [shards(): lax.all_to_all(outgoing, 'replica', split_axis=0, concat_axis=2, tiled=True)]
    ppermute x0 -> x12, starting transfers between devices: none -> 10.7 us  [exchange(): return lax.ppermute(value, axis, [(i, i ^ mask) for i in range(size)])]
    pallas_call x0 -> x1, Pallas kernels: none -> 7.51 us  [project(): pl.pallas_call(functools.partial(project_kernel, (tensors, replicas, line...]
  transfers between devices with their start and end apart: 2 -> 13, of which waited for: 1 -> 8; matrix products, arithmetic and copies ran while one was open for 1% -> 9% of each run, Pallas kernels for 0% -> 0%
where the time goes in v1:
time: 66.7 us; the launch traced here: 66.3 us
  waiting for transfers between devices  20.7 us (31%)
  starting transfers between devices  18 us (27%)
  local copies, waits for them, and re-layouts  8.39 us (13%)
  Pallas kernels  7.51 us (11%)
  other arithmetic  6.29 us (9%)
  matrix products  4.44 us (7%)
  between operations  0.97 us (1%)
    ppermute x12, waiting for transfers between devices, exchange(): return lax.ppermute(value, axis, [(i, i ^ mask) for i in range(size)])  17.9 us
    ppermute x12, starting transfers between devices, exchange(): return lax.ppermute(value, axis, [(i, i ^ mask) for i in range(size)])  10.7 us
    pallas_call x1, Pallas kernels, project(): pl.pallas_call(functools.partial(project_kernel, (tensors, replicas, line...  7.51 us
    all_to_all x1, starting transfers between devices, move_sums(): lax.all_to_all(split, 'replica', split_axis=0, concat_axis=0, tiled=True)  7.31 us
    all_to_all x1, waiting for transfers between devices, move_sums(): lax.all_to_all(split, 'replica', split_axis=0, concat_axis=0, tiled=True)  2.81 us
    dot_general x1, matrix products, attend(): jnp.einsum('tbgqd,bgcd->tbgqc', grouped, cache_keys, preferred_element_ty...  2.21 us
    reshape x1, local copies, waits for them, and re-layouts, move_sums(): split.transpose(2, 0, 1, 3)  2.12 us
    transpose x1, local copies, waits for them, and re-layouts, move_sums(): split.transpose(2, 0, 1, 3)  1.91 us
  transfers between devices with their start and end apart: 13, of which 8 were waited for; matrix products, arithmetic and copies ran while one was open for 9% of the time, Pallas kernels for 0%

profile of v1, /device:TPU:0, one launch (start us, length us, event | category | flops | bytes accessed | tf_op | source)
XLA Modules:
  0.0 66.3 jit_solution(8921508308063680514)
XLA Ops:
  0.6 0.0 copy-start
  0.7 0.9 %iota_compare_fusion = pred[4,1536]{1,0:T(4,128)(4,1)S(1)} fusion(s32[4]{0:T(128)} %param.17), kind=kLoop, calls=%fused_computation.74 | loop fusion | flops 6144 | bytes 6160 | tf_op jit(solution)/shard_map/lt | solution.py:27
  1.5 1.3 %fusion.62 = (f32[4,4,2,8]{3,0,2,1:T(4,128)S(1)}, f32[4,4,2,8,4]{3,4,0,2,1:T(4,128)S(1)}) fusion(bf16[4,4,2,128,1]{3,2,1,0,4:T(2,128)(2,1)} %bitcast.118, pred[4,4]{1,0:T(4,128)(4,1)S(1)} %iota_compare_fusion.2, bf16[4,4,16,128]{3,2,1,0:T(8,128)(2,1)} %param.12), kind=kOutput, calls=%fused_computation.111 | convolution fusion | flops 264960 | bytes 78864 | tf_op jit(solution)/shard_map/tbgqd,ubgd->tbgqu/dot_general | solution.py:30
  2.9 0.0 copy-start.3
  2.9 2.2 %fusion.61 = (f32[4,4,2,8]{3,0,2,1:T(4,128)S(1)}, f32[4,4,2,8,1536]{4,3,0,2,1:T(8,128)S(1)}) fusion(bf16[4,2,1536,128]{3,2,1,0:T(8,128)(2,1)S(1)} %copy-done, pred[4,1536]{1,0:T(4,128)(4,1)S(1)} %iota_compare_fusion, bf16[4,4,16,128]{3,2,1,0:T(8,128)(2,1)} %param.12), kind=kOutput, calls=%fused_computation.110 | convolution fusion | flops 101842688 | bytes 4791296 | tf_op jit(solution)/shard_map/tbgqd,bgcd->tbgqc/dot_general | solution.py:23
  5.1 0.0 copy-start.4
  5.1 0.1 fusion.50
  5.2 0.4 fusion.13
  5.6 0.2 copy-done.4
  5.8 0.2 fusion.51
  6.0 0.7 %fusion.20 = bf16[4,4,2,8,128]{4,3,0,2,1:T(8,128)(2,1)S(1)} fusion(f32[4,2,4,8,128]{4,3,2,1,0:T(8,128)S(1)} %fusion.51, bf16[4,2,1536,128]{3,2,1,0:T(8,128)(2,1)S(1)} %copy-done.3, f32[4,4,2,8,1536]{4,3,0,2,1:T(8,128)S(1)} %get-tuple-element.21, f32[4,4,2,8]{3,0,2,1:T(4,128)S(1)} %add.81, f32[4,4,2,8]{3,0,2,1:T(4,128)S(1)} %max.8), kind=kOutput, calls=%fused_computation.14 | convolution fusion | flops 101908480 | bytes 4917248 | tf_op jit(solution)/shard_map/tbgqc,bgcd->tbgqd/dot_general | solution.py:46
  6.7 0.0 copy-start.5
  6.7 0.0 copy-start.6
  6.8 1.2 %convert_element_type.119 = bf16[16,16,8,16]{3,2,1,0:T(8,128)(2,1)} reshape(bf16[4,4,2,8,128]{4,3,2,1,0:T(8,128)(2,1)S(1)} %copy.37) | data formatting | bytes 131072 | tf_op jit(solution)/shard_map/convert_element_type | solution.py:52
  7.9 1.9 %copy.38 = bf16[8,16,16,16]{3,2,1,0:T(8,128)(2,1)} copy(bf16[8,16,16,16]{3,0,2,1:T(8,128)(2,1)} %bitcast.115) | data formatting | bytes 131072 | tf_op jit(solution)/shard_map/transpose | solution.py:268
  9.8 2.1 %reshape.116 = bf16[8,16,256]{2,1,0:T(8,128)(2,1)} reshape(bf16[8,16,16,16]{3,2,1,0:T(8,128)(2,1)} %copy.38) | data formatting | bytes 131072 | tf_op jit(solution)/shard_map/reshape | solution.py:268
  12.0 7.3 %all-to-all-start = ((bf16[8,16,256]{2,1,0:T(8,128)(2,1)}), bf16[8,16,256]{2,1,0:T(8,128)(2,1)S(1)}, u32[]{:S(2)}, u32[]{:S(2)}) async-start(bf16[8,16,256]{2,1,0:T(8,128)(2,1)} %reshape.116), calls=%async_computation | async-start | bytes 131072 | tf_op jit(solution)/shard_map/all_to_all | solution.py:269
  19.4 0.1 dynamic-slice_compare_fusion
  19.5 0.1 dynamic-slice_bitcast_fusion
  19.6 0.2 convert_reduce_fusion
  19.7 0.1 dynamic_slice.10
  19.8 0.1 broadcast_in_dim.56
  19.9 0.5 broadcast.150
  20.4 0.7 %reduce.3 = s32[32]{0:T(128)S(1)} reduce(s32[32,1]{0,1:T(1,128)S(1)} %copy-done.6, s32[]{:T(128)} %broadcast.150), dimensions={1}, to_apply=%param.19.reduce_sub_computation.3 | reduce | bytes 260 | tf_op args[9]
  21.1 0.1 gt.21
  21.2 0.1 slice.81
  21.3 0.1 slice.82
  21.3 0.1 slice.79
  21.4 0.1 gt.22
  21.6 0.1 broadcast_in_dim.54
  21.6 0.1 eq.67
  21.8 0.1 eq.74
  21.9 0.7 %and_convert_fusion.base_rows = bf16[32,8]{1,0:T(8,128)(2,1)} fusion(s32[8]{0:T(128)S(1)} %dynamic-slice_bitcast_fusion, s32[8]{0:T(128)S(1)} %dynamic_slice.10, s32[32]{0:T(128)S(1)} %slice.82, s32[32]{0:T(128)S(1)} %slice.79, pred[8]{0:T(512)(128)(4,1)S(1)} %dynamic-slice_compare_fusion), kind=kLoop, calls=%fused_computation.79 | loop fusion | flops 1280 | bytes 840 | tf_op jit(solution)/shard_map/convert_element_type | solution.py:140
  22.6 0.1 fusion.47
  22.7 0.1 and_and_fusion
  22.7 0.6 add_convert_fusion
  23.4 2.8 %all-to-all-done = bf16[8,16,256]{2,1,0:T(8,128)(2,1)S(1)} async-done(((bf16[8,16,256]{2,1,0:T(8,128)(2,1)}), bf16[8,16,256]{2,1,0:T(8,128)(2,1)S(1)}, u32[]{:S(2)}, u32[]{:S(2)}) %all-to-all-start) | async-done | bytes 65568 | tf_op jit(solution)/shard_map/all_to_all | solution.py:269
  26.2 0.6 copy-done.2
  26.8 7.5 %project.1 = (bf16[2,2,4,40,512]{4,3,2,1,0:T(8,128)(2,1)}, bf16[2,2,4,40,512]{4,3,2,1,0:T(8,128)(2,1)}, bf16[2,2,4,40,512]{4,3,2,1,0:T(8,128)(2,1)}, bf16[2,2,4,40,512]{4,3,2,1,0:T(8,128)(2,1)}) custom-call(s32[1]{0:T(128)} %bitcast.me_ref, bf16[128,256]{1,0:T(8,128)(2,1)} %bitcast.116, bf16[160,128]{1,0:T(8,128)(2,1)} %bitcast.117, ...), custom_call_target="tpu_custom_call" | custom-call | flops 671088640 | bytes 4194304 | tf_op jit(solution)/shard_map/project/pallas_call | solution.py:208
  34.3 0.0 collective-permute-start
  34.3 0.5 collective-permute-start.6
  34.8 1.8 %collective-permute-done = bf16[2,2,4,40,512]{4,3,2,1,0:T(8,128)(2,1)S(1)} collective-permute-done((bf16[2,2,4,40,512]{4,3,2,1,0:T(8,128)(2,1)}, bf16[2,2,4,40,512]{4,3,2,1,0:T(8,128)(2,1)S(1)}, u32[]{:S(2)}, u32[]{:S(2)}) %collective-permute-start) | collective-permute-done | bytes 655392 | tf_op jit(solution)/shard_map/ppermute | solution.py:238
  36.6 1.3 %convert_add_fusion.1 = f32[2,2,4,40,512]{4,3,2,1,0:T(8,128)S(1)} fusion(bf16[2,2,4,40,512]{4,3,2,1,0:T(8,128)(2,1)S(1)} %collective-permute-done, bf16[2,2,4,40,512]{4,3,2,1,0:T(8,128)(2,1)} %get-tuple-element.6), kind=kLoop, calls=%fused_computation.11 | loop fusion | flops 983040 | bytes 2621440 | tf_op jit(solution)/shard_map/add | solution.py:275
  38.0 1.5 %collective-permute-start.1 = (bf16[2,4,40,512]{3,2,1,0:T(8,128)(2,1)S(1)}, bf16[2,4,40,512]{3,2,1,0:T(8,128)(2,1)S(1)}, u32[]{:S(2)}, u32[]{:S(2)}) collective-permute-start(bf16[2,4,40,512]{3,2,1,0:T(8,128)(2,1)S(1)} %fusion.29), channel_id=1, source_target_pairs={{0,2},{1,3},{2,0},{3,1},{4,6},{5,7},{6,4},{7,5},{8,10},{9,11},{10,... | collective-permute-start | bytes 983048 | tf_op jit(solution)/shard_map/ppermute | solution.py:238
  39.6 0.2 convert_add_fusion
  39.8 0.5 collective-permute-start.7
  40.3 7.5 %collective-permute-done.1 = bf16[2,4,40,512]{3,2,1,0:T(8,128)(2,1)S(1)} collective-permute-done((bf16[2,4,40,512]{3,2,1,0:T(8,128)(2,1)S(1)}, bf16[2,4,40,512]{3,2,1,0:T(8,128)(2,1)S(1)}, u32[]{:S(2)}, u32[]{:S(2)}) %collective-permute-start.1) | collective-permute-done | bytes 327712 | tf_op jit(solution)/shard_map/ppermute | solution.py:238
  47.8 0.1 fusion.28
  48.0 0.5 collective-permute-start.2
  48.4 1.0 %collective-permute-done.7 = bf16[2,4,40,512]{3,2,1,0:T(8,128)(2,1)S(1)} collective-permute-done((bf16[2,4,40,512]{3,2,1,0:T(8,128)(2,1)S(1)}, bf16[2,4,40,512]{3,2,1,0:T(8,128)(2,1)S(1)}, u32[]{:S(2)}, u32[]{:S(2)}) %collective-permute-start.7) | collective-permute-done | bytes 327712 | tf_op jit(solution)/shard_map/ppermute | solution.py:238
  49.4 0.1 fusion.27
  49.5 0.6 collective-permute-start.8
  50.1 3.3 %collective-permute-done.2 = bf16[4,40,512]{2,1,0:T(8,128)(2,1)S(1)} collective-permute-done((bf16[4,40,512]{2,1,0:T(8,128)(2,1)S(1)}, bf16[4,40,512]{2,1,0:T(8,128)(2,1)S(1)}, u32[]{:S(2)}, u32[]{:S(2)}) %collective-permute-start.2) | collective-permute-done | bytes 163872 | tf_op jit(solution)/shard_map/ppermute | solution.py:238
  53.5 0.3 collective-permute-start.3
  53.8 1.7 %collective-permute-start.5 = (bf16[40,512]{1,0:T(8,128)(2,1)S(1)}, bf16[40,512]{1,0:T(8,128)(2,1)S(1)}, u32[]{:S(2)}, u32[]{:S(2)}) collective-permute-start(bf16[40,512]{1,0:T(8,128)(2,1)S(1)} %get-tuple-element.18), channel_id=1, source_target_pairs={{0,24},{4,28},{8,16},{12,20},{16,8},{20,12},{24,0},{28,4},{1,25},{... | collective-permute-start | bytes 122888 | tf_op jit(solution)/shard_map/ppermute | solution.py:238
  55.5 1.5 %collective-permute-start.4 = (bf16[40,512]{1,0:T(8,128)(2,1)S(1)}, bf16[40,512]{1,0:T(8,128)(2,1)S(1)}, u32[]{:S(2)}, u32[]{:S(2)}) collective-permute-start(bf16[40,512]{1,0:T(8,128)(2,1)S(1)} %get-tuple-element.19), channel_id=1, source_target_pairs={{0,16},{4,20},{8,24},{12,28},{16,0},{20,4},{24,8},{28,12},{1,17},{... | collective-permute-start | bytes 122888 | tf_op jit(solution)/shard_map/ppermute | solution.py:238
  57.1 1.2 %collective-permute-start.9 = (bf16[40,512]{1,0:T(8,128)(2,1)S(1)}, bf16[40,512]{1,0:T(8,128)(2,1)S(1)}, u32[]{:S(2)}, u32[]{:S(2)}) collective-permute-start(bf16[40,512]{1,0:T(8,128)(2,1)S(1)} %get-tuple-element.14), channel_id=1, source_target_pairs={{0,8},{4,12},{8,0},{12,4},{16,24},{20,28},{24,16},{28,20},{1,9},{5... | collective-permute-start | bytes 122888 | tf_op jit(solution)/shard_map/ppermute | solution.py:238
  58.3 1.7 %collective-permute-start.11 = (bf16[40,512]{1,0:T(8,128)(2,1)S(1)}, bf16[40,512]{1,0:T(8,128)(2,1)S(1)}, u32[]{:S(2)}, u32[]{:S(2)}) collective-permute-start(bf16[40,512]{1,0:T(8,128)(2,1)S(1)} %get-tuple-element.15), channel_id=1, source_target_pairs={{0,24},{4,28},{8,16},{12,20},{16,8},{20,12},{24,0},{28,4},{1,25},{... | collective-permute-start | bytes 122888 | tf_op jit(solution)/shard_map/ppermute | solution.py:238
  60.0 0.7 collective-permute-start.10
  60.7 1.4 %collective-permute-done.4 = bf16[40,512]{1,0:T(8,128)(2,1)S(1)} collective-permute-done((bf16[40,512]{1,0:T(8,128)(2,1)S(1)}, bf16[40,512]{1,0:T(8,128)(2,1)S(1)}, u32[]{:S(2)}, u32[]{:S(2)}) %collective-permute-start.4) | collective-permute-done | bytes 40992 | tf_op jit(solution)/shard_map/ppermute | solution.py:238
  62.1 2.0 %collective-permute-done.11 = bf16[40,512]{1,0:T(8,128)(2,1)S(1)} collective-permute-done((bf16[40,512]{1,0:T(8,128)(2,1)S(1)}, bf16[40,512]{1,0:T(8,128)(2,1)S(1)}, u32[]{:S(2)}, u32[]{:S(2)}) %collective-permute-start.11) | collective-permute-done | bytes 40992 | tf_op jit(solution)/shard_map/ppermute | solution.py:238
  64.1 0.9 %collective-permute-done.10 = bf16[40,512]{1,0:T(8,128)(2,1)S(1)} collective-permute-done((bf16[40,512]{1,0:T(8,128)(2,1)S(1)}, bf16[40,512]{1,0:T(8,128)(2,1)S(1)}, u32[]{:S(2)}, u32[]{:S(2)}) %collective-permute-start.10) | collective-permute-done | bytes 40992 | tf_op jit(solution)/shard_map/ppermute | solution.py:238
  65.0 0.6 fusion.44
  65.7 0.6 reshape.120
  (42 shorter events, 0.4 us)
Async XLA Ops:
  0.6 2.2 %copy-start = (bf16[4,2,1536,128]{3,2,1,0:T(8,128)(2,1)S(1)}, bf16[4,2,1536,128]{3,2,1,0:T(8,128)(2,1)}, u32[]{:S(2)}) copy-start(bf16[4,2,1536,128]{3,2,1,0:T(8,128)(2,1)} %param.13) | copy-start | bytes 9437188
  2.9 3.2 %copy-start.3 = (bf16[4,2,1536,128]{3,2,1,0:T(8,128)(2,1)S(1)}, bf16[4,2,1536,128]{3,2,1,0:T(8,128)(2,1)}, u32[]{:S(2)}) copy-start(bf16[4,2,1536,128]{3,2,1,0:T(8,128)(2,1)} %param.14) | copy-start | bytes 9437188
  5.1 0.7 %copy-start.4 = (bf16[4,4,2,128]{3,2,1,0:T(2,128)(2,1)S(1)}, bf16[4,4,2,128]{3,2,1,0:T(2,128)(2,1)}, u32[]{:S(2)}) copy-start(bf16[4,4,2,128]{3,2,1,0:T(2,128)(2,1)} %param.16) | copy-start | bytes 24580
  6.7 12.7 %copy-start.5 = (s32[32]{0:T(128)S(1)}, s32[32]{0:T(128)}, u32[]{:S(2)}) copy-start(s32[32]{0:T(128)} %param.18) | copy-start | bytes 388
  6.7 12.8 %copy-start.6 = (s32[32,1]{0,1:T(1,128)S(1)}, s32[32,1]{0,1:T(1,128)}, u32[]{:S(2)}) copy-start(s32[32,1]{0,1:T(1,128)} %param.19) | copy-start | bytes 388
  12.0 14.2 %all-to-all-start = ((bf16[8,16,256]{2,1,0:T(8,128)(2,1)}), bf16[8,16,256]{2,1,0:T(8,128)(2,1)S(1)}, u32[]{:S(2)}, u32[]{:S(2)}) async-start(bf16[8,16,256]{2,1,0:T(8,128)(2,1)} %reshape.116), calls=%async_computation | async-start | bytes 131072 | tf_op jit(solution)/shard_map/all_to_all | solution.py:269
  26.2 0.6 copy-start.2
  34.3 2.3 %collective-permute-start = (bf16[2,2,4,40,512]{4,3,2,1,0:T(8,128)(2,1)}, bf16[2,2,4,40,512]{4,3,2,1,0:T(8,128)(2,1)S(1)}, u32[]{:S(2)}, u32[]{:S(2)}) collective-permute-start(bf16[2,2,4,40,512]{4,3,2,1,0:T(8,128)(2,1)} %get-tuple-element.7), channel_id=1, source_target_pairs={{0,1},{1,0},{2,3},{3,2},{4,5},{5,4},{6,7},{7,6},{8,9},{9,8},{10,11... | collective-permute-start | bytes 1966088 | tf_op jit(solution)/shard_map/ppermute | solution.py:238
  34.3 5.2 %collective-permute-start.6 = (bf16[2,2,4,40,512]{4,3,2,1,0:T(8,128)(2,1)}, bf16[2,2,4,40,512]{4,3,2,1,0:T(8,128)(2,1)S(1)}, u32[]{:S(2)}, u32[]{:S(2)}) collective-permute-start(bf16[2,2,4,40,512]{4,3,2,1,0:T(8,128)(2,1)} %get-tuple-element.9), channel_id=1, source_target_pairs={{0,1},{1,0},{2,3},{3,2},{4,5},{5,4},{6,7},{7,6},{8,9},{9,8},{10,11... | collective-permute-start | bytes 1966088 | tf_op jit(solution)/shard_map/ppermute | solution.py:238
  36.6 2.9 %copy-start.1 = (bf16[2,2,4,40,512]{4,3,2,1,0:T(8,128)(2,1)S(1)}, bf16[2,2,4,40,512]{4,3,2,1,0:T(8,128)(2,1)}, u32[]{:S(2)}) copy-start(bf16[2,2,4,40,512]{4,3,2,1,0:T(8,128)(2,1)} %get-tuple-element.8) | copy-start | bytes 1966084
  38.0 9.8 %collective-permute-start.1 = (bf16[2,4,40,512]{3,2,1,0:T(8,128)(2,1)S(1)}, bf16[2,4,40,512]{3,2,1,0:T(8,128)(2,1)S(1)}, u32[]{:S(2)}, u32[]{:S(2)}) collective-permute-start(bf16[2,4,40,512]{3,2,1,0:T(8,128)(2,1)S(1)} %fusion.29), channel_id=1, source_target_pairs={{0,2},{1,3},{2,0},{3,1},{4,6},{5,7},{6,4},{7,5},{8,10},{9,11},{10,... | collective-permute-start | bytes 983048 | tf_op jit(solution)/shard_map/ppermute | solution.py:238
  39.8 9.5 %collective-permute-start.7 = (bf16[2,4,40,512]{3,2,1,0:T(8,128)(2,1)S(1)}, bf16[2,4,40,512]{3,2,1,0:T(8,128)(2,1)S(1)}, u32[]{:S(2)}, u32[]{:S(2)}) collective-permute-start(bf16[2,4,40,512]{3,2,1,0:T(8,128)(2,1)S(1)} %fusion.30), channel_id=1, source_target_pairs={{0,4},{4,0},{8,12},{12,8},{16,20},{20,16},{24,28},{28,24},{1,5},{5... | collective-permute-start | bytes 983048 | tf_op jit(solution)/shard_map/ppermute | solution.py:238
  48.0 5.5 %collective-permute-start.2 = (bf16[4,40,512]{2,1,0:T(8,128)(2,1)S(1)}, bf16[4,40,512]{2,1,0:T(8,128)(2,1)S(1)}, u32[]{:S(2)}, u32[]{:S(2)}) collective-permute-start(bf16[4,40,512]{2,1,0:T(8,128)(2,1)S(1)} %fusion.33), channel_id=1, source_target_pairs={{0,4},{4,0},{8,12},{12,8},{16,20},{20,16},{24,28},{28,24},{1,5},{5... | collective-permute-start | bytes 491528 | tf_op jit(solution)/shard_map/ppermute | solution.py:238
  49.5 7.5 %collective-permute-start.8 = (bf16[4,40,512]{2,1,0:T(8,128)(2,1)S(1)}, bf16[4,40,512]{2,1,0:T(8,128)(2,1)S(1)}, u32[]{:S(2)}, u32[]{:S(2)}) collective-permute-start(bf16[4,40,512]{2,1,0:T(8,128)(2,1)S(1)} %fusion.34), channel_id=1, source_target_pairs={{0,2},{1,3},{2,0},{3,1},{4,6},{5,7},{6,4},{7,5},{8,10},{9,11},{10,... | collective-permute-start | bytes 491528 | tf_op jit(solution)/shard_map/ppermute | solution.py:238
  53.5 6.5 %collective-permute-start.3 = (bf16[40,512]{1,0:T(8,128)(2,1)S(1)}, bf16[40,512]{1,0:T(8,128)(2,1)S(1)}, u32[]{:S(2)}, u32[]{:S(2)}) collective-permute-start(bf16[40,512]{1,0:T(8,128)(2,1)S(1)} %get-tuple-element.17), channel_id=1, source_target_pairs={{0,8},{4,12},{8,0},{12,4},{16,24},{20,28},{24,16},{28,20},{1,9},{5... | collective-permute-start | bytes 122888 | tf_op jit(solution)/shard_map/ppermute | solution.py:238
  53.8 6.9 %collective-permute-start.5 = (bf16[40,512]{1,0:T(8,128)(2,1)S(1)}, bf16[40,512]{1,0:T(8,128)(2,1)S(1)}, u32[]{:S(2)}, u32[]{:S(2)}) collective-permute-start(bf16[40,512]{1,0:T(8,128)(2,1)S(1)} %get-tuple-element.18), channel_id=1, source_target_pairs={{0,24},{4,28},{8,16},{12,20},{16,8},{20,12},{24,0},{28,4},{1,25},{... | collective-permute-start | bytes 122888 | tf_op jit(solution)/shard_map/ppermute | solution.py:238
  55.5 6.6 %collective-permute-start.4 = (bf16[40,512]{1,0:T(8,128)(2,1)S(1)}, bf16[40,512]{1,0:T(8,128)(2,1)S(1)}, u32[]{:S(2)}, u32[]{:S(2)}) collective-permute-start(bf16[40,512]{1,0:T(8,128)(2,1)S(1)} %get-tuple-element.19), channel_id=1, source_target_pairs={{0,16},{4,20},{8,24},{12,28},{16,0},{20,4},{24,8},{28,12},{1,17},{... | collective-permute-start | bytes 122888 | tf_op jit(solution)/shard_map/ppermute | solution.py:238
  57.1 5.0 %collective-permute-start.9 = (bf16[40,512]{1,0:T(8,128)(2,1)S(1)}, bf16[40,512]{1,0:T(8,128)(2,1)S(1)}, u32[]{:S(2)}, u32[]{:S(2)}) collective-permute-start(bf16[40,512]{1,0:T(8,128)(2,1)S(1)} %get-tuple-element.14), channel_id=1, source_target_pairs={{0,8},{4,12},{8,0},{12,4},{16,24},{20,28},{24,16},{28,20},{1,9},{5... | collective-permute-start | bytes 122888 | tf_op jit(solution)/shard_map/ppermute | solution.py:238
  58.3 5.8 %collective-permute-start.11 = (bf16[40,512]{1,0:T(8,128)(2,1)S(1)}, bf16[40,512]{1,0:T(8,128)(2,1)S(1)}, u32[]{:S(2)}, u32[]{:S(2)}) collective-permute-start(bf16[40,512]{1,0:T(8,128)(2,1)S(1)} %get-tuple-element.15), channel_id=1, source_target_pairs={{0,24},{4,28},{8,16},{12,20},{16,8},{20,12},{24,0},{28,4},{1,25},{... | collective-permute-start | bytes 122888 | tf_op jit(solution)/shard_map/ppermute | solution.py:238
  60.0 4.9 %collective-permute-start.10 = (bf16[40,512]{1,0:T(8,128)(2,1)S(1)}, bf16[40,512]{1,0:T(8,128)(2,1)S(1)}, u32[]{:S(2)}, u32[]{:S(2)}) collective-permute-start(bf16[40,512]{1,0:T(8,128)(2,1)S(1)} %get-tuple-element.16), channel_id=1, source_target_pairs={{0,16},{4,20},{8,24},{12,28},{16,0},{20,4},{24,8},{28,12},{1,17},{... | collective-permute-start | bytes 122888 | tf_op jit(solution)/shard_map/ppermute | solution.py:238

commit v2 on v0

--- a/solution.py
+++ b/solution.py
@@ -1,11 +1,15 @@
+import functools
 import math
 
 import jax
 import jax.numpy as jnp
 from jax import lax
+from jax.experimental import pallas as pl
+from jax.experimental.pallas import tpu as pltpu
 from jax.sharding import PartitionSpec as P
 
 SLOT_DEV = 1
+LANES = 128
 
 
 def attend(queries, cache_keys, cache_values, new_keys, new_values, lengths):
@@ -55,7 +59,7 @@
     return lax.dynamic_slice_in_dim(totals, lax.axis_index("tensor") * share, share, 1)
 
 
-def shards(
+def regroup_weight(
     base_stream,
     out_weight,
     queries,
@@ -102,6 +106,306 @@
     return (updates, trainer_rows)
 
 
+def attend_kernel(scale, lengths, queries, new_keys, new_values, keys, values, out, held, fresh_k, fresh_v, turned, sems):
+    steps_count, row_count, heads_here, head_size = queries.shape
+    kv_here, positions_count = keys.shape[1], keys.shape[2]
+    group = heads_here // kv_here
+    lines = steps_count * group
+    f32 = jnp.float32
+    fetches = [
+        pltpu.make_async_copy(values.at[i], held.at[i], sems.at[i]) for i in range(row_count)
+    ]
+    for fetch in fetches:
+        fetch.start()
+    fresh_k[...] = jnp.zeros_like(fresh_k)
+    fresh_v[...] = jnp.zeros_like(fresh_v)
+    place = lax.broadcasted_iota(jnp.int32, (lines, positions_count), 1)
+    fresh_at = lax.broadcasted_iota(jnp.int32, (lines, LANES), 1)
+    fresh_step = lax.broadcasted_iota(jnp.int32, (lines, LANES), 0) // group
+    fresh_valid = fresh_at <= fresh_step
+    width = head_size // group
+    lane = lax.broadcasted_iota(jnp.int32, (group, head_size), 1) // width
+    diagonal = (lane - lax.broadcasted_iota(jnp.int32, (group, head_size), 0)) & (group - 1)
+    turn = (((1,), (1,)), ((), ()))
+    for i in range(row_count):
+        is_valid = place < lengths[i]
+        weighed = []
+        for g in range(kv_here):
+            query = jnp.concatenate(
+                [queries[t, i, g * group : (g + 1) * group] for t in range(steps_count)], axis=0
+            )
+            for t in range(steps_count):
+                fresh_k[g, t : t + 1] = new_keys[t, i, g : g + 1]
+                fresh_v[g, t : t + 1] = new_values[t, i, g : g + 1]
+            scores = lax.dot_general(query, keys[i, g], turn, preferred_element_type=f32) * scale
+            scores = jnp.where(is_valid, scores, f32(-1e30))
+            fresh = lax.dot_general(query, fresh_k[g], turn, preferred_element_type=f32) * scale
+            fresh = jnp.where(fresh_valid, fresh, f32(-1e30))
+            highest = jnp.maximum(
+                jnp.max(scores, axis=1, keepdims=True), jnp.max(fresh, axis=1, keepdims=True)
+            )
+            scores = jnp.exp(scores - highest)
+            fresh = jnp.exp(fresh - highest)
+            total = jnp.sum(scores, axis=1, keepdims=True) + jnp.sum(fresh, axis=1, keepdims=True)
+            share = 1.0 / total
+            weighed.append(
+                ((scores * share).astype(jnp.bfloat16), (fresh * share).astype(jnp.bfloat16))
+            )
+        fetches[i].wait()
+        for g in range(kv_here):
+            probs, fresh_probs = weighed[g]
+            mixed = jnp.dot(probs, held[i, g], preferred_element_type=f32)
+            mixed = mixed + jnp.dot(fresh_probs, fresh_v[g], preferred_element_type=f32)
+            for t in range(steps_count):
+                part = mixed[t * group : (t + 1) * group]
+                moved = jnp.where(diagonal == 0, part, 0.0)
+                for d in range(1, group):
+                    rolled = pltpu.roll(pltpu.roll(part, group - d, 0), d * width, 1)
+                    moved = jnp.where(diagonal == d, rolled, moved)
+                turned[g, pl.ds(t * row_count + i, group, stride=steps_count * row_count), :] = moved
+    for g in range(kv_here):
+        out[:, g * head_size : (g + 1) * head_size] = turned[g].astype(jnp.bfloat16)
+
+
+def in_vmem(*arrays):
+    return [pltpu.with_memory_space_constraint(v, pltpu.VMEM) for v in arrays]
+
+
+def attend_split(queries, cache_keys, cache_values, new_keys, new_values, lengths):
+    steps_count, row_count, heads_here, head_size = queries.shape
+    _, kv_here, positions_count, _ = cache_keys.shape
+    group = heads_here // kv_here
+    lines = steps_count * row_count
+    vmem = pl.BlockSpec(memory_space=pltpu.VMEM)
+    out = pl.pallas_call(
+        functools.partial(attend_kernel, 1.0 / math.sqrt(head_size)),
+        out_shape=pltpu.VMEM((group * lines, kv_here * head_size), jnp.bfloat16),
+        in_specs=[
+            pl.BlockSpec(memory_space=pltpu.SMEM),
+            vmem,
+            vmem,
+            vmem,
+            vmem,
+            pl.BlockSpec(memory_space=pl.ANY),
+        ],
+        out_specs=vmem,
+        scratch_shapes=[
+            pltpu.VMEM(cache_values.shape, jnp.bfloat16),
+            pltpu.VMEM((kv_here, LANES, head_size), jnp.bfloat16),
+            pltpu.VMEM((kv_here, LANES, head_size), jnp.bfloat16),
+            pltpu.VMEM((kv_here, group * lines, head_size), jnp.float32),
+            pltpu.SemaphoreType.DMA((row_count,)),
+        ],
+        compiler_params=pltpu.CompilerParams(vmem_limit_bytes=16 * 2**20),
+        cost_estimate=pl.CostEstimate(
+            flops=4 * lines * heads_here * positions_count * head_size,
+            bytes_accessed=4 * row_count * kv_here * positions_count * head_size,
+            transcendentals=lines * heads_here * positions_count,
+        ),
+        name="attend",
+    )(lengths, *in_vmem(queries, new_keys, new_values, cache_keys), cache_values)
+    return out.reshape(group, lines, kv_here * head_size)
+
+
+def select_kernel(sizes, me, owners, finished, rows, base_rows):
+    tensors, replicas, steps_count, row_count = sizes
+    total_rows = replicas * row_count
+    share = total_rows // tensors
+    lines = steps_count * share
+    me_r, me_t = me[0], me[1]
+
+    def tell(row_of):
+        name, rank, done = (jnp.zeros_like(row_of) for _ in range(3))
+        for j in range(total_rows):
+            name = jnp.where(row_of == j, owners[j], name)
+            done = jnp.where(row_of == j, finished[j], done)
+        for j in range(total_rows):
+            rank = rank + jnp.where((name == owners[j]) & (row_of > j), 1, 0)
+        return jnp.where(done > 0, name, -1), rank
+
+    width = steps_count * total_rows
+    col = lax.broadcasted_iota(jnp.int32, (1, width), 1)
+    per = steps_count * row_count
+    row_of = col // per * row_count + (col & (row_count - 1))
+    step_of = (col & (per - 1)) // row_count
+    name, rank = tell(row_of)
+    own = lax.broadcasted_iota(jnp.int32, (1, LANES), 1)
+    base_name, base_rank = tell(own + me_t * share)
+    base_name = jnp.where(own < share, base_name, -1)
+    line = lax.broadcasted_iota(jnp.int32, (lines, width), 0)
+    line_row, line_step = line & (share - 1), line // share
+    owner = lax.broadcasted_iota(jnp.int32, (replicas, width), 0) ^ me_r
+    base_owner = lax.broadcasted_iota(jnp.int32, (replicas, LANES), 0) ^ me_r
+    picked = lambda hit: jnp.where(hit, 1.0, 0.0).astype(jnp.bfloat16)
+    for t in range(tensors):
+        target = me_t ^ t
+        hit = (row_of == target * share + line_row) & (step_of == line_step)
+        first = t * (lines + replicas)
+        rows[first : first + lines] = picked(hit)
+        hit = (name == owner) & (rank == target)
+        rows[first + lines : first + lines + replicas] = picked(hit)
+        hit = (base_name == base_owner) & (base_rank == target)
+        base_rows[t * replicas : (t + 1) * replicas] = picked(hit)[:, :share]
+
+
+def select_rows(owners, finished, steps_count, row_count):
+    replicas, tensors = lax.axis_size("replica"), lax.axis_size("tensor")
+    me = jnp.stack([lax.axis_index("replica"), lax.axis_index("tensor")]).astype(jnp.int32)
+    share = replicas * row_count // tensors
+    smem, vmem = pl.BlockSpec(memory_space=pltpu.SMEM), pl.BlockSpec(memory_space=pltpu.VMEM)
+    height = tensors * (steps_count * share + replicas)
+    return pl.pallas_call(
+        functools.partial(select_kernel, (tensors, replicas, steps_count, row_count)),
+        out_shape=(
+            pltpu.VMEM((height, steps_count * replicas * row_count), jnp.bfloat16),
+            pltpu.VMEM((tensors * replicas, share), jnp.bfloat16),
+        ),
+        in_specs=[smem, smem, smem],
+        out_specs=[vmem, vmem],
+        compiler_params=pltpu.CompilerParams(vmem_limit_bytes=4 * 2**20),
+        cost_estimate=pl.CostEstimate(flops=10**6, bytes_accessed=10**5, transcendentals=0),
+        name="select",
+    )(me, owners[:, 0], finished)
+
+
+def project_kernel(sizes, part, me_ref, gathered, rows, base_rows, base, weight, keep, send, slot_sums):
+    tensors, replicas, lines = sizes
+    f32 = jnp.float32
+    me = me_ref[0]
+    half = keep.shape[-1]
+    held = jnp.dot(rows[...], gathered[...], preferred_element_type=f32).astype(jnp.bfloat16)
+    tall = lines + replicas
+    extra = jnp.dot(
+        base_rows[...], base[:, part * half : (part + 1) * half], preferred_element_type=f32
+    )
+
+    def at(t, r):
+        ref = send if t % 2 else keep
+        return ref.at[(t // 2, r % 2, r // 2) if part == 0 else (r % 2, t // 2, r // 2)]
+
+    for r in range(replicas):
+        block = r ^ me
+        first_col = pl.multiple_of((block * 2 + part) * half, half)
+        sums = jnp.dot(held, weight[:, pl.ds(first_col, half)], preferred_element_type=f32)
+        for t in range(tensors):
+            first = t * tall
+            at(t, r)[:lines] = sums[first : first + lines].astype(jnp.bfloat16)
+            slot = sums[first + lines : first + tall]
+            if r == 0:
+                slot = slot + extra[t * replicas : (t + 1) * replicas]
+            for c in range(half // LANES):
+                slot_sums[t, c, pl.ds(block, replicas, stride=replicas), :] = slot[
+                    :, c * LANES : (c + 1) * LANES
+                ]
+    for t in range(tensors):
+        for r in range(replicas):
+            for c in range(half // LANES):
+                at(t, r)[lines:, c * LANES : (c + 1) * LANES] = slot_sums[
+                    t, c, r * replicas : (r + 1) * replicas
+                ].astype(jnp.bfloat16)
+
+
+def project(part, gathered, rows, base_rows, base_stream, weight):
+    replicas, tensors = lax.axis_size("replica"), lax.axis_size("tensor")
+    depth, model = weight.shape
+    half = model // replicas // 2
+    tall = rows.shape[0] // tensors
+    me = lax.axis_index("replica").astype(jnp.int32).reshape(1)
+    lead = (tensors // 2, 2) if part == 0 else (2, tensors // 2)
+    shape = pltpu.VMEM(lead + (replicas // 2, tall, half), jnp.bfloat16)
+    smem, vmem = pl.BlockSpec(memory_space=pltpu.SMEM), pl.BlockSpec(memory_space=pltpu.VMEM)
+    return pl.pallas_call(
+        functools.partial(project_kernel, (tensors, replicas, tall - replicas), part),
+        out_shape=(shape, shape),
+        in_specs=[smem] + [vmem] * 5,
+        out_specs=(vmem, vmem),
+        scratch_shapes=[
+            pltpu.VMEM((tensors, half // LANES, replicas * replicas, LANES), jnp.float32),
+        ],
+        compiler_params=pltpu.CompilerParams(vmem_limit_bytes=8 * 2**20),
+        cost_estimate=pl.CostEstimate(
+            flops=rows.shape[0] * depth * model,
+            bytes_accessed=depth * model,
+            transcendentals=0,
+        ),
+        name=f"project_{part}",
+    )(me, *in_vmem(gathered, rows, base_rows, base_stream, weight))
+
+
+def exchange(value, axis, mask):
+    size = lax.axis_size(axis)
+    return lax.ppermute(value, axis, [(i, i ^ mask) for i in range(size)])
+
+
+def reduce_scatter(keep, send, stages):
+    f32 = jnp.float32
+    came = [exchange(send, *stages[0])]
+
+    def part(*at):
+        terms = [keep[at]] + [v[at[i:]] for i, v in enumerate(came)]
+        return functools.reduce(jnp.add, [v.astype(f32) for v in terms])
+
+    last = keep.shape[2]
+    came.append(exchange(part(1).astype(jnp.bfloat16), *stages[1]))
+    came.append(exchange(part(0, 1).astype(jnp.bfloat16), *stages[2]))
+    moved = [
+        exchange(part(0, 0, m).astype(jnp.bfloat16), stages[3][0], stages[3][1] * m)
+        for m in range(1, last)
+    ]
+    result = functools.reduce(jnp.add, [part(0, 0, 0)] + [v.astype(f32) for v in moved])
+    return result.astype(jnp.bfloat16)
+
+
+def move_sums(
+    base_stream,
+    out_weight,
+    queries,
+    cache_keys,
+    cache_values,
+    new_keys,
+    new_values,
+    lengths,
+    finished,
+    owners,
+):
+    steps_count, row_count, heads_here, head_size = queries.shape
+    replicas, tensors = lax.axis_size("replica"), lax.axis_size("tensor")
+    model = out_weight.shape[2]
+    share = replicas * row_count // tensors
+    lines = steps_count * share
+    split = attend_split(queries, cache_keys, cache_values, new_keys, new_values, lengths)
+    gathered = lax.all_to_all(split, "replica", split_axis=0, concat_axis=0, tiled=True)
+    gathered = gathered.reshape(-1, gathered.shape[2])
+    rows, base_rows = select_rows(owners, finished, steps_count, row_count)
+    weight = out_weight.reshape(-1, model)
+    operands = (gathered, rows, base_rows, base_stream, weight)
+    core, across = ("tensor", 1), ("tensor", 2)
+    beside, along = ("replica", 1), ("replica", 2)
+    total = jnp.concatenate(
+        [
+            reduce_scatter(*project(0, *operands), (core, across, beside, along)),
+            reduce_scatter(*project(1, *operands), (core, beside, across, along)),
+        ],
+        axis=1,
+    )
+    updates = total[:lines].reshape(steps_count, share, model // replicas)
+    trainer_rows = total[lines:].reshape(1, SLOT_DEV, model)
+    return (updates, trainer_rows)
+
+
+def shards(*arrays):
+    out_weight, queries, cache_keys = arrays[1:4]
+    steps_count, row_count, heads_here, head_size = queries.shape
+    replicas, tensors = lax.axis_size("replica"), lax.axis_size("tensor")
+    sent = steps_count * row_count * replicas
+    few = sent <= heads_here * out_weight.shape[1]
+    group = heads_here // cache_keys.shape[1]
+    shares = replicas * row_count // tensors
+    powers = all(n & (n - 1) == 0 for n in (replicas, steps_count, row_count, shares))
+    fits = tensors == 4 and replicas == group == 8 and powers and head_size == LANES
+    return (move_sums if few and fits else regroup_weight)(*arrays)
+
+
 def solution(mesh):
     placed = (
         P("tensor", "replica"),

time: 321 us -> 60 us (0.19)
  blocking collectives: 130 us -> 0 us
  local copies, waits for them, and re-layouts: 125 us -> 9.49 us
  between operations: 14.2 us -> 0.74 us
  starting transfers between devices: 7.48 us -> 19.1 us
  waiting for transfers between devices: 31.9 us -> 22.3 us
  matrix products: 7.07 us -> 0 us
  Pallas kernels: 0 us -> 6.72 us
    all_gather x2 -> x0, blocking collectives: 118 us -> none  [the longest x1 113 us: shards(): lax.all_gather(attended, 'replica', axis=1, tiled=True)]
    unnamed x25 -> x20, local copies, waits for them, and re-layouts: 92 us -> 8.86 us
    all_to_all x1 -> x0, local copies, waits for them, and re-layouts: 32.9 us -> none  [shards(): lax.all_to_all(out_weight, 'replica', split_axis=2, concat_axis=1, tiled=...]
    psum x1 -> x0, waiting for transfers between devices: 31.9 us -> none  [reduce_heads(): totals = lax.psum(rounded, 'tensor').astype(jnp.float32)]
    ppermute x0 -> x12, waiting for transfers between devices: none -> 16.1 us  [exchange(): return lax.ppermute(value, axis, [(i, i ^ mask) for i in range(size)])]
    all_to_all x1 -> x0, blocking collectives: 11.9 us -> none  [shards(): lax.all_to_all(outgoing, 'replica', split_axis=0, concat_axis=2, tiled=True)]
    ppermute x0 -> x12, starting transfers between devices: none -> 11.8 us  [exchange(): return lax.ppermute(value, axis, [(i, i ^ mask) for i in range(size)])]
    dot_general x6 -> x0, matrix products: 7.07 us -> none  [the longest x1 4.24 us: shards(): jnp.einsum('tbf,fc->tbc', lax.all_gather(attended, 'replica', axis=1, til...]
  transfers between devices with their start and end apart: 2 -> 13, of which waited for: 1 -> 8; matrix products, arithmetic and copies ran while one was open for 1% -> 1% of each run, Pallas kernels for 0% -> 2%
where the time goes in v2:
time: 60 us; the launch traced here: 59.6 us
  waiting for transfers between devices  22.3 us (37%)
  starting transfers between devices  19.1 us (32%)
  local copies, waits for them, and re-layouts  9.49 us (16%)
  Pallas kernels  6.72 us (11%)
  other arithmetic  1.24 us (2%)
  between operations  0.74 us (1%)
    ppermute x12, waiting for transfers between devices, exchange(): return lax.ppermute(value, axis, [(i, i ^ mask) for i in range(size)])  16.1 us
    ppermute x12, starting transfers between devices, exchange(): return lax.ppermute(value, axis, [(i, i ^ mask) for i in range(size)])  11.8 us
    unnamed x20, local copies, waits for them, and re-layouts  8.86 us
    all_to_all x1, starting transfers between devices, move_sums(): lax.all_to_all(split, 'replica', split_axis=0, concat_axis=0, tiled=True)  7.32 us
    all_to_all x1, waiting for transfers between devices, move_sums(): lax.all_to_all(split, 'replica', split_axis=0, concat_axis=0, tiled=True)  6.16 us
    pallas_call x1, Pallas kernels, attend_split(): pl.pallas_call(functools.partial(attend_kernel, 1.0 / math.sqrt(head_size...  4.69 us
    pallas_call x2, Pallas kernels, project(): pl.pallas_call(functools.partial(project_kernel, (tensors, replicas, tall...  1.37 us
  transfers between devices with their start and end apart: 13, of which 8 were waited for; matrix products, arithmetic and copies ran while one was open for 1% of the time, Pallas kernels for 2%

profile of v2, /device:TPU:0, one launch (start us, length us, event | category | flops | bytes accessed | tf_op | source)
XLA Modules:
  0.0 59.6 jit_solution(797962168969297042)
XLA Ops:
  0.6 0.0 copy-start.1
  0.6 1.9 %copy-done.1 = bf16[4,2,1536,128]{3,2,1,0:T(8,128)(2,1)S(1)} copy-done((bf16[4,2,1536,128]{3,2,1,0:T(8,128)(2,1)S(1)}, bf16[4,2,1536,128]{3,2,1,0:T(8,128)(2,1)}, u32[]{:S(2)}) %copy-start.1) | copy-done | bytes 3145752
  2.5 0.0 copy-start.2
  2.5 1.9 %copy-done.2 = bf16[4,2,1536,128]{3,2,1,0:T(8,128)(2,1)S(1)} copy-done((bf16[4,2,1536,128]{3,2,1,0:T(8,128)(2,1)S(1)}, bf16[4,2,1536,128]{3,2,1,0:T(8,128)(2,1)}, u32[]{:S(2)}) %copy-start.2) | copy-done | bytes 3145752
  4.4 0.0 copy-start.3
  4.4 0.8 %copy-done.3 = bf16[4,4,16,128]{3,2,1,0:T(8,128)(2,1)S(1)} copy-done((bf16[4,4,16,128]{3,2,1,0:T(8,128)(2,1)S(1)}, bf16[4,4,16,128]{3,2,1,0:T(8,128)(2,1)}, u32[]{:S(2)}) %copy-start.3) | copy-done | bytes 65560
  5.3 0.0 copy-start.5
  5.3 0.7 %copy-done.5 = bf16[4,4,2,128]{3,2,1,0:T(2,128)(2,1)S(1)} copy-done((bf16[4,4,2,128]{3,2,1,0:T(2,128)(2,1)S(1)}, bf16[4,4,2,128]{3,2,1,0:T(2,128)(2,1)}, u32[]{:S(2)}) %copy-start.5) | copy-done | bytes 8216
  6.0 0.0 copy-start.6
  6.0 0.7 %copy-done.6 = bf16[4,4,2,128]{3,2,1,0:T(2,128)(2,1)S(1)} copy-done((bf16[4,4,2,128]{3,2,1,0:T(2,128)(2,1)S(1)}, bf16[4,4,2,128]{3,2,1,0:T(2,128)(2,1)}, u32[]{:S(2)}) %copy-start.6) | copy-done | bytes 8216
  6.6 0.0 copy-start.7
  6.7 0.7 %copy-done.7 = s32[4]{0:T(128)S(1)} copy-done((s32[4]{0:T(128)S(1)}, s32[4]{0:T(128)}, u32[]{:S(2)}) %copy-start.7) | copy-done | bytes 40
  7.3 0.0 copy-start.8
  7.3 0.0 copy-start.9
  7.3 0.0 copy-start.4
  7.3 4.7 %attend.1 = bf16[128,256]{1,0:T(8,128)(2,1)} custom-call(s32[4]{0:T(128)S(1)} %copy-done.7, bf16[4,4,16,128]{3,2,1,0:T(8,128)(2,1)S(1)} %copy-done.3, bf16[4,4,2,128]{3,2,1,0:T(2,128)(2,1)S(1)} %copy-done.5, bf16[4,4,2,128]{3,2,1,0:T(2,128)(2,1)S(1)} %copy-done.6, bf16[4,2,1536,128]{3,2,1,0:T(8,128)(2,1)S(1)} %copy-done.1, ...), custom_call_target="tpu_custom_call" | custom-call | flops 201326592 | bytes 6291456 | tf_op jit(solution)/shard_map/attend/pallas_call | solution.py:180
  12.0 7.3 %all-to-all-start = ((bf16[8,16,256]{2,1,0:T(8,128)(2,1)}), bf16[8,16,256]{2,1,0:T(8,128)(2,1)S(1)}, u32[]{:S(2)}, u32[]{:S(2)}) async-start(bf16[8,16,256]{2,1,0:T(8,128)(2,1)} %bitcast.1), calls=%async_computation | async-start | bytes 131072 | tf_op jit(solution)/shard_map/all_to_all | solution.py:377
  19.3 0.1 pad_add_fusion.me
  19.4 0.0 copy-done.8
  19.4 0.0 copy-done.9
  19.4 0.7 %select.1 = (bf16[160,128]{1,0:T(8,128)(2,1)S(1)}, bf16[32,8]{1,0:T(8,128)(2,1)S(1)}) custom-call(s32[2]{0:T(128)S(1)} %pad_add_fusion.me, s32[32]{0:T(128)S(1)} %bitcast.126, s32[32]{0:T(128)S(1)} %copy-done.9), custom_call_target="tpu_custom_call" | custom-call | flops 1000000 | bytes 100000 | tf_op jit(solution)/shard_map/select/pallas_call | solution.py:257
  20.1 6.2 %all-to-all-done = bf16[8,16,256]{2,1,0:T(8,128)(2,1)S(1)} async-done(((bf16[8,16,256]{2,1,0:T(8,128)(2,1)}), bf16[8,16,256]{2,1,0:T(8,128)(2,1)S(1)}, u32[]{:S(2)}, u32[]{:S(2)}) %all-to-all-start) | async-done | bytes 65568 | tf_op jit(solution)/shard_map/all_to_all | solution.py:377
  26.2 0.0 copy-done.4
  26.2 0.0 copy-start
  26.2 2.2 %copy-done = bf16[16,16,8192]{2,1,0:T(8,128)(2,1)S(1)} copy-done((bf16[16,16,8192]{2,1,0:T(8,128)(2,1)S(1)}, bf16[16,16,8192]{2,1,0:T(8,128)(2,1)}, u32[]{:S(2)}) %copy-start) | copy-done | bytes 4194328
  28.4 0.7 %project_1.1 = (bf16[2,2,4,40,512]{4,3,2,1,0:T(8,128)(2,1)S(1)}, bf16[2,2,4,40,512]{4,3,2,1,0:T(8,128)(2,1)S(1)}) custom-call(s32[1]{0:T(128)} %bitcast.me_ref, bf16[128,256]{1,0:T(8,128)(2,1)S(1)} %bitcast.124, bf16[160,128]{1,0:T(8,128)(2,1)S(1)} %get-tuple-element.8.rows, bf16[32,8]{1,0:T(8,128)(2,1)S(1)} %get-tuple-element.9.base_rows, ...), custom_call_target="tpu_custom_call" | custom-call | flops 335544320 | bytes 2097152 | tf_op jit(solution)/shard_map/project_1/pallas_call | solution.py:317
  29.1 0.1 collective-permute-start.6
  29.2 0.7 %project_0.1 = (bf16[2,2,4,40,512]{4,3,2,1,0:T(8,128)(2,1)S(1)}, bf16[2,2,4,40,512]{4,3,2,1,0:T(8,128)(2,1)S(1)}) custom-call(s32[1]{0:T(128)} %bitcast.me_ref, bf16[128,256]{1,0:T(8,128)(2,1)S(1)} %bitcast.125, bf16[160,128]{1,0:T(8,128)(2,1)S(1)} %get-tuple-element.8.rows, bf16[32,8]{1,0:T(8,128)(2,1)S(1)} %get-tuple-element.9.base_rows, ...), custom_call_target="tpu_custom_call" | custom-call | flops 335544320 | bytes 2097152 | tf_op jit(solution)/shard_map/project_0/pallas_call | solution.py:317
  29.9 0.6 collective-permute-start
  30.4 0.8 %collective-permute-done.6 = bf16[2,2,4,40,512]{4,3,2,1,0:T(8,128)(2,1)S(1)} collective-permute-done((bf16[2,2,4,40,512]{4,3,2,1,0:T(8,128)(2,1)S(1)}, bf16[2,2,4,40,512]{4,3,2,1,0:T(8,128)(2,1)S(1)}, u32[]{:S(2)}, u32[]{:S(2)}) %collective-permute-start.6) | collective-permute-done | bytes 655392 | tf_op jit(solution)/shard_map/ppermute | solution.py:337
  31.3 0.1 fusion.1
  31.4 0.5 collective-permute-start.7
  31.8 0.4 collective-permute-done
  32.2 0.1 fusion
  32.3 1.6 %collective-permute-start.1 = (bf16[2,4,40,512]{3,2,1,0:T(8,128)(2,1)S(1)}, bf16[2,4,40,512]{3,2,1,0:T(8,128)(2,1)S(1)}, u32[]{:S(2)}, u32[]{:S(2)}) collective-permute-start(bf16[2,4,40,512]{3,2,1,0:T(8,128)(2,1)S(1)} %fusion), channel_id=1, source_target_pairs={{0,2},{1,3},{2,0},{3,1},{4,6},{5,7},{6,4},{7,5},{8,10},{9,11},{10,... | collective-permute-start | bytes 983048 | tf_op jit(solution)/shard_map/ppermute | solution.py:337
  33.9 7.3 %collective-permute-done.7 = bf16[2,4,40,512]{3,2,1,0:T(8,128)(2,1)S(1)} collective-permute-done((bf16[2,4,40,512]{3,2,1,0:T(8,128)(2,1)S(1)}, bf16[2,4,40,512]{3,2,1,0:T(8,128)(2,1)S(1)}, u32[]{:S(2)}, u32[]{:S(2)}) %collective-permute-start.7) | collective-permute-done | bytes 327712 | tf_op jit(solution)/shard_map/ppermute | solution.py:337
  41.2 0.1 fusion.2
  41.3 1.6 %collective-permute-start.8 = (bf16[4,40,512]{2,1,0:T(8,128)(2,1)S(1)}, bf16[4,40,512]{2,1,0:T(8,128)(2,1)S(1)}, u32[]{:S(2)}, u32[]{:S(2)}) collective-permute-start(bf16[4,40,512]{2,1,0:T(8,128)(2,1)S(1)} %fusion.2), channel_id=1, source_target_pairs={{0,2},{1,3},{2,0},{3,1},{4,6},{5,7},{6,4},{7,5},{8,10},{9,11},{10,... | collective-permute-start | bytes 491528 | tf_op jit(solution)/shard_map/ppermute | solution.py:337
  42.8 0.0 collective-permute-done.1
  42.8 0.1 fusion.3
  42.9 0.5 collective-permute-start.2
  43.4 3.4 %collective-permute-done.8 = bf16[4,40,512]{2,1,0:T(8,128)(2,1)S(1)} collective-permute-done((bf16[4,40,512]{2,1,0:T(8,128)(2,1)S(1)}, bf16[4,40,512]{2,1,0:T(8,128)(2,1)S(1)}, u32[]{:S(2)}, u32[]{:S(2)}) %collective-permute-start.8) | collective-permute-done | bytes 163872 | tf_op jit(solution)/shard_map/ppermute | solution.py:337
  46.7 0.1 fusion.6
  46.8 0.3 collective-permute-start.9
  47.1 1.7 %collective-permute-start.11 = (bf16[40,512]{1,0:T(8,128)(2,1)S(1)}, bf16[40,512]{1,0:T(8,128)(2,1)S(1)}, u32[]{:S(2)}, u32[]{:S(2)}) collective-permute-start(bf16[40,512]{1,0:T(8,128)(2,1)S(1)} %get-tuple-element.15), channel_id=1, source_target_pairs={{0,24},{4,28},{8,16},{12,20},{16,8},{20,12},{24,0},{28,4},{1,25},{... | collective-permute-start | bytes 122888 | tf_op jit(solution)/shard_map/ppermute | solution.py:337
  48.8 1.5 %collective-permute-start.10 = (bf16[40,512]{1,0:T(8,128)(2,1)S(1)}, bf16[40,512]{1,0:T(8,128)(2,1)S(1)}, u32[]{:S(2)}, u32[]{:S(2)}) collective-permute-start(bf16[40,512]{1,0:T(8,128)(2,1)S(1)} %get-tuple-element.16), channel_id=1, source_target_pairs={{0,16},{4,20},{8,24},{12,28},{16,0},{20,4},{24,8},{28,12},{1,17},{... | collective-permute-start | bytes 122888 | tf_op jit(solution)/shard_map/ppermute | solution.py:337
  50.3 0.0 collective-permute-done.2
  50.3 0.1 fusion.13
  50.4 1.2 %collective-permute-start.3 = (bf16[40,512]{1,0:T(8,128)(2,1)S(1)}, bf16[40,512]{1,0:T(8,128)(2,1)S(1)}, u32[]{:S(2)}, u32[]{:S(2)}) collective-permute-start(bf16[40,512]{1,0:T(8,128)(2,1)S(1)} %get-tuple-element.17), channel_id=1, source_target_pairs={{0,8},{4,12},{8,0},{12,4},{16,24},{20,28},{24,16},{28,20},{1,9},{5... | collective-permute-start | bytes 122888 | tf_op jit(solution)/shard_map/ppermute | solution.py:337
  51.6 1.7 %collective-permute-start.5 = (bf16[40,512]{1,0:T(8,128)(2,1)S(1)}, bf16[40,512]{1,0:T(8,128)(2,1)S(1)}, u32[]{:S(2)}, u32[]{:S(2)}) collective-permute-start(bf16[40,512]{1,0:T(8,128)(2,1)S(1)} %get-tuple-element.18), channel_id=1, source_target_pairs={{0,24},{4,28},{8,16},{12,20},{16,8},{20,12},{24,0},{28,4},{1,25},{... | collective-permute-start | bytes 122888 | tf_op jit(solution)/shard_map/ppermute | solution.py:337
  53.3 0.0 collective-permute-done.9
  53.3 0.6 %collective-permute-start.4 = (bf16[40,512]{1,0:T(8,128)(2,1)S(1)}, bf16[40,512]{1,0:T(8,128)(2,1)S(1)}, u32[]{:S(2)}, u32[]{:S(2)}) collective-permute-start(bf16[40,512]{1,0:T(8,128)(2,1)S(1)} %get-tuple-element.19), channel_id=1, source_target_pairs={{0,16},{4,20},{8,24},{12,28},{16,0},{20,4},{24,8},{28,12},{1,17},{... | collective-permute-start | bytes 122888 | tf_op jit(solution)/shard_map/ppermute | solution.py:337
  54.0 0.0 collective-permute-done.11
  54.0 1.4 %collective-permute-done.10 = bf16[40,512]{1,0:T(8,128)(2,1)S(1)} collective-permute-done((bf16[40,512]{1,0:T(8,128)(2,1)S(1)}, bf16[40,512]{1,0:T(8,128)(2,1)S(1)}, u32[]{:S(2)}, u32[]{:S(2)}) %collective-permute-start.10) | collective-permute-done | bytes 40992 | tf_op jit(solution)/shard_map/ppermute | solution.py:337
  55.4 0.0 collective-permute-done.3
  55.4 2.0 %collective-permute-done.5 = bf16[40,512]{1,0:T(8,128)(2,1)S(1)} collective-permute-done((bf16[40,512]{1,0:T(8,128)(2,1)S(1)}, bf16[40,512]{1,0:T(8,128)(2,1)S(1)}, u32[]{:S(2)}, u32[]{:S(2)}) %collective-permute-start.5) | collective-permute-done | bytes 40992 | tf_op jit(solution)/shard_map/ppermute | solution.py:337
  57.4 0.9 %collective-permute-done.4 = bf16[40,512]{1,0:T(8,128)(2,1)S(1)} collective-permute-done((bf16[40,512]{1,0:T(8,128)(2,1)S(1)}, bf16[40,512]{1,0:T(8,128)(2,1)S(1)}, u32[]{:S(2)}, u32[]{:S(2)}) %collective-permute-start.4) | collective-permute-done | bytes 40992 | tf_op jit(solution)/shard_map/ppermute | solution.py:337
  58.3 0.6 %fusion.19 = bf16[4,8,1024]{2,1,0:T(8,128)(2,1)} fusion(bf16[40,512]{1,0:T(8,128)(2,1)S(1)} %fusion.17, bf16[40,512]{1,0:T(8,128)(2,1)S(1)} %fusion.10), kind=kLoop, calls=%fused_computation.43 | loop fusion | flops 131072 | bytes 147456 | tf_op jit(solution)/shard_map/reshape | solution.py:391
  59.0 0.6 %reshape.102 = bf16[1,1,8192]{2,1,0:T(2,128)(2,1)} reshape(bf16[8,1024]{1,0:T(8,128)(2,1)S(1)} %pad_maximum_fusion) | data formatting | bytes 32768 | tf_op jit(solution)/shard_map/reshape | solution.py:392
  (3 shorter events, 0.1 us)
Async XLA Ops:
  0.6 1.9 %copy-start.1 = (bf16[4,2,1536,128]{3,2,1,0:T(8,128)(2,1)S(1)}, bf16[4,2,1536,128]{3,2,1,0:T(8,128)(2,1)}, u32[]{:S(2)}) copy-start(bf16[4,2,1536,128]{3,2,1,0:T(8,128)(2,1)} %keys.1) | copy-start | bytes 9437188
  2.5 1.9 %copy-start.2 = (bf16[4,2,1536,128]{3,2,1,0:T(8,128)(2,1)S(1)}, bf16[4,2,1536,128]{3,2,1,0:T(8,128)(2,1)}, u32[]{:S(2)}) copy-start(bf16[4,2,1536,128]{3,2,1,0:T(8,128)(2,1)} %values.1) | copy-start | bytes 9437188
  4.4 0.8 %copy-start.3 = (bf16[4,4,16,128]{3,2,1,0:T(8,128)(2,1)S(1)}, bf16[4,4,16,128]{3,2,1,0:T(8,128)(2,1)}, u32[]{:S(2)}) copy-start(bf16[4,4,16,128]{3,2,1,0:T(8,128)(2,1)} %queries.1) | copy-start | bytes 196612
  5.3 0.7 %copy-start.5 = (bf16[4,4,2,128]{3,2,1,0:T(2,128)(2,1)S(1)}, bf16[4,4,2,128]{3,2,1,0:T(2,128)(2,1)}, u32[]{:S(2)}) copy-start(bf16[4,4,2,128]{3,2,1,0:T(2,128)(2,1)} %new_keys.1) | copy-start | bytes 24580
  6.0 0.7 %copy-start.6 = (bf16[4,4,2,128]{3,2,1,0:T(2,128)(2,1)S(1)}, bf16[4,4,2,128]{3,2,1,0:T(2,128)(2,1)}, u32[]{:S(2)}) copy-start(bf16[4,4,2,128]{3,2,1,0:T(2,128)(2,1)} %new_values.1) | copy-start | bytes 24580
  6.6 0.7 %copy-start.7 = (s32[4]{0:T(128)S(1)}, s32[4]{0:T(128)}, u32[]{:S(2)}) copy-start(s32[4]{0:T(128)} %lengths.1) | copy-start | bytes 52
  7.3 12.1 %copy-start.8 = (s32[32,1]{0,1:T(1,128)S(1)}, s32[32,1]{0,1:T(1,128)}, u32[]{:S(2)}) copy-start(s32[32,1]{0,1:T(1,128)} %param.19) | copy-start | bytes 388
  7.3 12.1 %copy-start.9 = (s32[32]{0:T(128)S(1)}, s32[32]{0:T(128)}, u32[]{:S(2)}) copy-start(s32[32]{0:T(128)} %finished.1) | copy-start | bytes 388
  7.3 18.9 %copy-start.4 = (bf16[8,1024]{1,0:T(8,128)(2,1)S(1)}, bf16[8,1024]{1,0:T(8,128)(2,1)}, u32[]{:S(2)}) copy-start(bf16[8,1024]{1,0:T(8,128)(2,1)} %base.3) | copy-start | bytes 49156
  12.0 14.2 %all-to-all-start = ((bf16[8,16,256]{2,1,0:T(8,128)(2,1)}), bf16[8,16,256]{2,1,0:T(8,128)(2,1)S(1)}, u32[]{:S(2)}, u32[]{:S(2)}) async-start(bf16[8,16,256]{2,1,0:T(8,128)(2,1)} %bitcast.1), calls=%async_computation | async-start | bytes 131072 | tf_op jit(solution)/shard_map/all_to_all | solution.py:377
  26.2 2.2 %copy-start = (bf16[16,16,8192]{2,1,0:T(8,128)(2,1)S(1)}, bf16[16,16,8192]{2,1,0:T(8,128)(2,1)}, u32[]{:S(2)}) copy-start(bf16[16,16,8192]{2,1,0:T(8,128)(2,1)} %param.11) | copy-start | bytes 12582916
  29.1 2.2 %collective-permute-start.6 = (bf16[2,2,4,40,512]{4,3,2,1,0:T(8,128)(2,1)S(1)}, bf16[2,2,4,40,512]{4,3,2,1,0:T(8,128)(2,1)S(1)}, u32[]{:S(2)}, u32[]{:S(2)}) collective-permute-start(bf16[2,2,4,40,512]{4,3,2,1,0:T(8,128)(2,1)S(1)} %get-tuple-element.13), channel_id=1, source_target_pairs={{0,1},{1,0},{2,3},{3,2},{4,5},{5,4},{6,7},{7,6},{8,9},{9,8},{10,11... | collective-permute-start | bytes 1966088 | tf_op jit(solution)/shard_map/ppermute | solution.py:337
  29.9 2.3 %collective-permute-start = (bf16[2,2,4,40,512]{4,3,2,1,0:T(8,128)(2,1)S(1)}, bf16[2,2,4,40,512]{4,3,2,1,0:T(8,128)(2,1)S(1)}, u32[]{:S(2)}, u32[]{:S(2)}) collective-permute-start(bf16[2,2,4,40,512]{4,3,2,1,0:T(8,128)(2,1)S(1)} %get-tuple-element.11), channel_id=1, source_target_pairs={{0,1},{1,0},{2,3},{3,2},{4,5},{5,4},{6,7},{7,6},{8,9},{9,8},{10,11... | collective-permute-start | bytes 1966088 | tf_op jit(solution)/shard_map/ppermute | solution.py:337
  31.4 9.8 %collective-permute-start.7 = (bf16[2,4,40,512]{3,2,1,0:T(8,128)(2,1)S(1)}, bf16[2,4,40,512]{3,2,1,0:T(8,128)(2,1)S(1)}, u32[]{:S(2)}, u32[]{:S(2)}) collective-permute-start(bf16[2,4,40,512]{3,2,1,0:T(8,128)(2,1)S(1)} %fusion.1), channel_id=1, source_target_pairs={{0,4},{4,0},{8,12},{12,8},{16,20},{20,16},{24,28},{28,24},{1,5},{5... | collective-permute-start | bytes 983048 | tf_op jit(solution)/shard_map/ppermute | solution.py:337
  32.3 10.5 %collective-permute-start.1 = (bf16[2,4,40,512]{3,2,1,0:T(8,128)(2,1)S(1)}, bf16[2,4,40,512]{3,2,1,0:T(8,128)(2,1)S(1)}, u32[]{:S(2)}, u32[]{:S(2)}) collective-permute-start(bf16[2,4,40,512]{3,2,1,0:T(8,128)(2,1)S(1)} %fusion), channel_id=1, source_target_pairs={{0,2},{1,3},{2,0},{3,1},{4,6},{5,7},{6,4},{7,5},{8,10},{9,11},{10,... | collective-permute-start | bytes 983048 | tf_op jit(solution)/shard_map/ppermute | solution.py:337
  41.3 5.5 %collective-permute-start.8 = (bf16[4,40,512]{2,1,0:T(8,128)(2,1)S(1)}, bf16[4,40,512]{2,1,0:T(8,128)(2,1)S(1)}, u32[]{:S(2)}, u32[]{:S(2)}) collective-permute-start(bf16[4,40,512]{2,1,0:T(8,128)(2,1)S(1)} %fusion.2), channel_id=1, source_target_pairs={{0,2},{1,3},{2,0},{3,1},{4,6},{5,7},{6,4},{7,5},{8,10},{9,11},{10,... | collective-permute-start | bytes 491528 | tf_op jit(solution)/shard_map/ppermute | solution.py:337
  42.9 7.4 %collective-permute-start.2 = (bf16[4,40,512]{2,1,0:T(8,128)(2,1)S(1)}, bf16[4,40,512]{2,1,0:T(8,128)(2,1)S(1)}, u32[]{:S(2)}, u32[]{:S(2)}) collective-permute-start(bf16[4,40,512]{2,1,0:T(8,128)(2,1)S(1)} %fusion.3), channel_id=1, source_target_pairs={{0,4},{4,0},{8,12},{12,8},{16,20},{20,16},{24,28},{28,24},{1,5},{5... | collective-permute-start | bytes 491528 | tf_op jit(solution)/shard_map/ppermute | solution.py:337
  46.8 6.5 %collective-permute-start.9 = (bf16[40,512]{1,0:T(8,128)(2,1)S(1)}, bf16[40,512]{1,0:T(8,128)(2,1)S(1)}, u32[]{:S(2)}, u32[]{:S(2)}) collective-permute-start(bf16[40,512]{1,0:T(8,128)(2,1)S(1)} %get-tuple-element.14), channel_id=1, source_target_pairs={{0,8},{4,12},{8,0},{12,4},{16,24},{20,28},{24,16},{28,20},{1,9},{5... | collective-permute-start | bytes 122888 | tf_op jit(solution)/shard_map/ppermute | solution.py:337
  47.1 6.9 %collective-permute-start.11 = (bf16[40,512]{1,0:T(8,128)(2,1)S(1)}, bf16[40,512]{1,0:T(8,128)(2,1)S(1)}, u32[]{:S(2)}, u32[]{:S(2)}) collective-permute-start(bf16[40,512]{1,0:T(8,128)(2,1)S(1)} %get-tuple-element.15), channel_id=1, source_target_pairs={{0,24},{4,28},{8,16},{12,20},{16,8},{20,12},{24,0},{28,4},{1,25},{... | collective-permute-start | bytes 122888 | tf_op jit(solution)/shard_map/ppermute | solution.py:337
  48.8 6.6 %collective-permute-start.10 = (bf16[40,512]{1,0:T(8,128)(2,1)S(1)}, bf16[40,512]{1,0:T(8,128)(2,1)S(1)}, u32[]{:S(2)}, u32[]{:S(2)}) collective-permute-start(bf16[40,512]{1,0:T(8,128)(2,1)S(1)} %get-tuple-element.16), channel_id=1, source_target_pairs={{0,16},{4,20},{8,24},{12,28},{16,0},{20,4},{24,8},{28,12},{1,17},{... | collective-permute-start | bytes 122888 | tf_op jit(solution)/shard_map/ppermute | solution.py:337
  50.4 5.0 %collective-permute-start.3 = (bf16[40,512]{1,0:T(8,128)(2,1)S(1)}, bf16[40,512]{1,0:T(8,128)(2,1)S(1)}, u32[]{:S(2)}, u32[]{:S(2)}) collective-permute-start(bf16[40,512]{1,0:T(8,128)(2,1)S(1)} %get-tuple-element.17), channel_id=1, source_target_pairs={{0,8},{4,12},{8,0},{12,4},{16,24},{20,28},{24,16},{28,20},{1,9},{5... | collective-permute-start | bytes 122888 | tf_op jit(solution)/shard_map/ppermute | solution.py:337
  51.6 5.8 %collective-permute-start.5 = (bf16[40,512]{1,0:T(8,128)(2,1)S(1)}, bf16[40,512]{1,0:T(8,128)(2,1)S(1)}, u32[]{:S(2)}, u32[]{:S(2)}) collective-permute-start(bf16[40,512]{1,0:T(8,128)(2,1)S(1)} %get-tuple-element.18), channel_id=1, source_target_pairs={{0,24},{4,28},{8,16},{12,20},{16,8},{20,12},{24,0},{28,4},{1,25},{... | collective-permute-start | bytes 122888 | tf_op jit(solution)/shard_map/ppermute | solution.py:337
  53.3 4.9 %collective-permute-start.4 = (bf16[40,512]{1,0:T(8,128)(2,1)S(1)}, bf16[40,512]{1,0:T(8,128)(2,1)S(1)}, u32[]{:S(2)}, u32[]{:S(2)}) collective-permute-start(bf16[40,512]{1,0:T(8,128)(2,1)S(1)} %get-tuple-element.19), channel_id=1, source_target_pairs={{0,16},{4,20},{8,24},{12,28},{16,0},{20,4},{24,8},{28,12},{1,17},{... | collective-permute-start | bytes 122888 | tf_op jit(solution)/shard_map/ppermute | solution.py:337

commit v3 on v2

--- a/solution.py
+++ b/solution.py
@@ -106,17 +106,26 @@
     return (updates, trainer_rows)
 
 
-def attend_kernel(scale, lengths, queries, new_keys, new_values, keys, values, out, held, fresh_k, fresh_v, turned, sems):
+def attend_kernel(scale, *refs):
+    sources, out, places, (fresh_k, fresh_v, turned, sems) = refs[:6], refs[6], refs[7:13], refs[13:]
+    lengths, queries, new_keys, new_values, keys, held = places
     steps_count, row_count, heads_here, head_size = queries.shape
     kv_here, positions_count = keys.shape[1], keys.shape[2]
     group = heads_here // kv_here
     lines = steps_count * group
     f32 = jnp.float32
-    fetches = [
-        pltpu.make_async_copy(values.at[i], held.at[i], sems.at[i]) for i in range(row_count)
-    ]
-    for fetch in fetches:
-        fetch.start()
+    small = [pltpu.make_async_copy(sources[n], places[n], sems.at[n]) for n in range(4)]
+    fetch = lambda n, i: pltpu.make_async_copy(
+        sources[4 + n].at[i], places[4 + n].at[i], sems.at[4 + n * row_count + i]
+    )
+    fetches = [(fetch(0, i), fetch(1, i)) for i in range(row_count)]
+    fetches[0][0].start()
+    for copy in small:
+        copy.start()
+    fetches[0][1].start()
+    for pair in fetches[1:]:
+        pair[0].start()
+        pair[1].start()
     fresh_k[...] = jnp.zeros_like(fresh_k)
     fresh_v[...] = jnp.zeros_like(fresh_v)
     place = lax.broadcasted_iota(jnp.int32, (lines, positions_count), 1)
@@ -127,7 +136,10 @@
     lane = lax.broadcasted_iota(jnp.int32, (group, head_size), 1) // width
     diagonal = (lane - lax.broadcasted_iota(jnp.int32, (group, head_size), 0)) & (group - 1)
     turn = (((1,), (1,)), ((), ()))
+    for copy in small:
+        copy.wait()
     for i in range(row_count):
+        fetches[i][0].wait()
         is_valid = place < lengths[i]
         weighed = []
         for g in range(kv_here):
@@ -151,7 +163,7 @@
             weighed.append(
                 ((scores * share).astype(jnp.bfloat16), (fresh * share).astype(jnp.bfloat16))
             )
-        fetches[i].wait()
+        fetches[i][1].wait()
         for g in range(kv_here):
             probs, fresh_probs = weighed[g]
             mixed = jnp.dot(probs, held[i, g], preferred_element_type=f32)
@@ -176,25 +188,20 @@
     _, kv_here, positions_count, _ = cache_keys.shape
     group = heads_here // kv_here
     lines = steps_count * row_count
+    operands = (lengths, queries, new_keys, new_values, cache_keys, cache_values)
     vmem = pl.BlockSpec(memory_space=pltpu.VMEM)
-    out = pl.pallas_call(
+    (out,) = pl.pallas_call(
         functools.partial(attend_kernel, 1.0 / math.sqrt(head_size)),
-        out_shape=pltpu.VMEM((group * lines, kv_here * head_size), jnp.bfloat16),
-        in_specs=[
-            pl.BlockSpec(memory_space=pltpu.SMEM),
-            vmem,
-            vmem,
-            vmem,
-            vmem,
-            pl.BlockSpec(memory_space=pl.ANY),
-        ],
-        out_specs=vmem,
+        out_shape=(pltpu.VMEM((group * lines, kv_here * head_size), jnp.bfloat16),),
+        in_specs=[pl.BlockSpec(memory_space=pltpu.HBM)] * len(operands),
+        out_specs=(vmem,),
         scratch_shapes=[
-            pltpu.VMEM(cache_values.shape, jnp.bfloat16),
+            pltpu.SMEM(lengths.shape, lengths.dtype),
+            *(pltpu.VMEM(v.shape, v.dtype) for v in operands[1:]),
             pltpu.VMEM((kv_here, LANES, head_size), jnp.bfloat16),
             pltpu.VMEM((kv_here, LANES, head_size), jnp.bfloat16),
             pltpu.VMEM((kv_here, group * lines, head_size), jnp.float32),
-            pltpu.SemaphoreType.DMA((row_count,)),
+            pltpu.SemaphoreType.DMA((4 + 2 * row_count,)),
         ],
         compiler_params=pltpu.CompilerParams(vmem_limit_bytes=16 * 2**20),
         cost_estimate=pl.CostEstimate(
@@ -203,16 +210,35 @@
             transcendentals=lines * heads_here * positions_count,
         ),
         name="attend",
-    )(lengths, *in_vmem(queries, new_keys, new_values, cache_keys), cache_values)
+    )(*[pltpu.with_memory_space_constraint(v, pltpu.HBM) for v in operands])
     return out.reshape(group, lines, kv_here * head_size)
 
 
-def select_kernel(sizes, me, owners, finished, rows, base_rows):
+def fetch_weight(weight, held, sems, me, part, blocks):
+    if not blocks:
+        return []
+    half = held.shape[1] // len(blocks)
+    return [
+        pltpu.make_async_copy(
+            weight.at[:, pl.ds(pl.multiple_of(((r ^ me) * 2 + part) * half, half), half)],
+            held.at[:, pl.ds(n * half, half)],
+            sems.at[n],
+        )
+        for n, r in enumerate(blocks)
+    ]
+
+
+def select_kernel(sizes, me, owners, finished, weight, rows, base_rows, early, late, *sems):
     tensors, replicas, steps_count, row_count = sizes
     total_rows = replicas * row_count
     share = total_rows // tensors
     lines = steps_count * share
     me_r, me_t = me[0], me[1]
+    blocks = range(replicas)
+    fetches = fetch_weight(weight, early, sems[0], me_r, 1, blocks)
+    fetches += fetch_weight(weight, late, sems[1], me_r, 0, blocks[: replicas // 2])
+    for fetch in fetches:
+        fetch.start()
 
     def tell(row_of):
         name, rank, done = (jnp.zeros_like(row_of) for _ in range(3))
@@ -246,33 +272,49 @@
         rows[first + lines : first + lines + replicas] = picked(hit)
         hit = (base_name == base_owner) & (base_rank == target)
         base_rows[t * replicas : (t + 1) * replicas] = picked(hit)[:, :share]
-
-
-def select_rows(owners, finished, steps_count, row_count):
+    for fetch in fetches:
+        fetch.wait()
+
+
+def select_rows(owners, finished, weight, steps_count, row_count):
     replicas, tensors = lax.axis_size("replica"), lax.axis_size("tensor")
     me = jnp.stack([lax.axis_index("replica"), lax.axis_index("tensor")]).astype(jnp.int32)
     share = replicas * row_count // tensors
     smem, vmem = pl.BlockSpec(memory_space=pltpu.SMEM), pl.BlockSpec(memory_space=pltpu.VMEM)
     height = tensors * (steps_count * share + replicas)
+    depth, model = weight.shape
     return pl.pallas_call(
         functools.partial(select_kernel, (tensors, replicas, steps_count, row_count)),
         out_shape=(
             pltpu.VMEM((height, steps_count * replicas * row_count), jnp.bfloat16),
             pltpu.VMEM((tensors * replicas, share), jnp.bfloat16),
+            pltpu.VMEM((depth, model // 2), weight.dtype),
+            pltpu.VMEM((depth, model // 4), weight.dtype),
         ),
-        in_specs=[smem, smem, smem],
-        out_specs=[vmem, vmem],
+        in_specs=[smem, smem, smem, pl.BlockSpec(memory_space=pltpu.HBM)],
+        out_specs=[vmem] * 4,
+        scratch_shapes=[
+            pltpu.SemaphoreType.DMA((replicas,)),
+            pltpu.SemaphoreType.DMA((replicas // 2,)),
+        ],
         compiler_params=pltpu.CompilerParams(vmem_limit_bytes=4 * 2**20),
-        cost_estimate=pl.CostEstimate(flops=10**6, bytes_accessed=10**5, transcendentals=0),
+        cost_estimate=pl.CostEstimate(
+            flops=10**6, bytes_accessed=2 * weight.size, transcendentals=0
+        ),
         name="select",
-    )(me, owners[:, 0], finished)
-
-
-def project_kernel(sizes, part, me_ref, gathered, rows, base_rows, base, weight, keep, send, slot_sums):
+    )(me, owners[:, 0], finished, weight)
+
+
+def project_kernel(sizes, part, me_ref, weight, *refs):
+    gathered, rows, base_rows, base, first_weight, keep, send, slot_sums, rest, sems = refs
     tensors, replicas, lines = sizes
     f32 = jnp.float32
     me = me_ref[0]
     half = keep.shape[-1]
+    near = first_weight.shape[1] // half
+    fetches = fetch_weight(weight, rest, sems, me, part, range(near, replicas))
+    for fetch in fetches:
+        fetch.start()
     held = jnp.dot(rows[...], gathered[...], preferred_element_type=f32).astype(jnp.bfloat16)
     tall = lines + replicas
     extra = jnp.dot(
@@ -285,8 +327,12 @@
 
     for r in range(replicas):
         block = r ^ me
-        first_col = pl.multiple_of((block * 2 + part) * half, half)
-        sums = jnp.dot(held, weight[:, pl.ds(first_col, half)], preferred_element_type=f32)
+        if r < near:
+            columns = first_weight[:, r * half : (r + 1) * half]
+        else:
+            fetches[r - near].wait()
+            columns = rest[:, (r - near) * half : (r - near + 1) * half]
+        sums = jnp.dot(held, columns, preferred_element_type=f32)
         for t in range(tensors):
             first = t * tall
             at(t, r)[:lines] = sums[first : first + lines].astype(jnp.bfloat16)
@@ -305,10 +351,11 @@
                 ].astype(jnp.bfloat16)
 
 
-def project(part, gathered, rows, base_rows, base_stream, weight):
+def project(part, gathered, rows, base_rows, base_stream, first_weight, weight):
     replicas, tensors = lax.axis_size("replica"), lax.axis_size("tensor")
     depth, model = weight.shape
     half = model // replicas // 2
+    missing = max(1, replicas - first_weight.shape[1] // half)
     tall = rows.shape[0] // tensors
     me = lax.axis_index("replica").astype(jnp.int32).reshape(1)
     lead = (tensors // 2, 2) if part == 0 else (2, tensors // 2)
@@ -317,10 +364,12 @@
     return pl.pallas_call(
         functools.partial(project_kernel, (tensors, replicas, tall - replicas), part),
         out_shape=(shape, shape),
-        in_specs=[smem] + [vmem] * 5,
+        in_specs=[smem, pl.BlockSpec(memory_space=pltpu.HBM)] + [vmem] * 5,
         out_specs=(vmem, vmem),
         scratch_shapes=[
             pltpu.VMEM((tensors, half // LANES, replicas * replicas, LANES), jnp.float32),
+            pltpu.VMEM((depth, missing * half), weight.dtype),
+            pltpu.SemaphoreType.DMA((missing,)),
         ],
         compiler_params=pltpu.CompilerParams(vmem_limit_bytes=8 * 2**20),
         cost_estimate=pl.CostEstimate(
@@ -329,7 +378,7 @@
             transcendentals=0,
         ),
         name=f"project_{part}",
-    )(me, *in_vmem(gathered, rows, base_rows, base_stream, weight))
+    )(me, weight, *in_vmem(gathered, rows, base_rows, base_stream, first_weight))
 
 
 def exchange(value, axis, mask):
@@ -337,23 +386,71 @@
     return lax.ppermute(value, axis, [(i, i ^ mask) for i in range(size)])
 
 
-def reduce_scatter(keep, send, stages):
-    f32 = jnp.float32
+def add_up(terms):
+    return functools.reduce(jnp.add, [v.astype(jnp.float32) for v in terms])
+
+
+def part_of(keep, came, *at):
+    return add_up([keep[at]] + [v[at[i:]] for i, v in enumerate(came)])
+
+
+def first_stages(keep, send, stages):
     came = [exchange(send, *stages[0])]
-
-    def part(*at):
-        terms = [keep[at]] + [v[at[i:]] for i, v in enumerate(came)]
-        return functools.reduce(jnp.add, [v.astype(f32) for v in terms])
-
-    last = keep.shape[2]
-    came.append(exchange(part(1).astype(jnp.bfloat16), *stages[1]))
-    came.append(exchange(part(0, 1).astype(jnp.bfloat16), *stages[2]))
-    moved = [
-        exchange(part(0, 0, m).astype(jnp.bfloat16), stages[3][0], stages[3][1] * m)
-        for m in range(1, last)
-    ]
-    result = functools.reduce(jnp.add, [part(0, 0, 0)] + [v.astype(f32) for v in moved])
-    return result.astype(jnp.bfloat16)
+    came.append(exchange(part_of(keep, came, 1).astype(jnp.bfloat16), *stages[1]))
+    came.append(exchange(part_of(keep, came, 0, 1).astype(jnp.bfloat16), *stages[2]))
+    return (keep, *came)
+
+
+def join_kernel(*refs):
+    halves, outs = (refs[:4], refs[4:8]), refs[8:]
+    half = refs[0].shape[-1]
+    for n, (keep, *came) in enumerate(halves):
+        for m, out in enumerate(outs):
+            total = part_of(keep, came, 0, 0, m)
+            out[:, n * half : (n + 1) * half] = total.astype(out.dtype)
+
+
+def join(first, second):
+    _, _, last, tall, half = first[0].shape
+    vmem = pl.BlockSpec(memory_space=pltpu.VMEM)
+    kinds = [jnp.float32] + [jnp.bfloat16] * (last - 1)
+    return pl.pallas_call(
+        join_kernel,
+        out_shape=[pltpu.VMEM((tall, 2 * half), kind) for kind in kinds],
+        in_specs=[vmem] * 8,
+        out_specs=[vmem] * last,
+        compiler_params=pltpu.CompilerParams(vmem_limit_bytes=4 * 2**20),
+        name="join",
+    )(*in_vmem(*first, *second))
+
+
+def finish_kernel(*refs):
+    terms, (updates, slots) = refs[:-2], refs[-2:]
+    total = add_up([v[...] for v in terms]).astype(jnp.bfloat16)
+    steps_count, share, cols = updates.shape
+    for t in range(steps_count):
+        updates[t] = total[t * share : (t + 1) * share]
+    slot = total[steps_count * share :]
+    for r in range(slot.shape[0]):
+        slots[0:1, r * cols : (r + 1) * cols] = slot[r : r + 1]
+
+
+def finish(steps_count, terms):
+    tall, cols = terms[0].shape
+    replicas = lax.axis_size("replica")
+    share = (tall - replicas) // steps_count
+    vmem = pl.BlockSpec(memory_space=pltpu.VMEM)
+    return pl.pallas_call(
+        finish_kernel,
+        out_shape=(
+            jax.ShapeDtypeStruct((steps_count, share, cols), jnp.bfloat16),
+            jax.ShapeDtypeStruct((1, replicas * cols), jnp.bfloat16),
+        ),
+        in_specs=[vmem] * len(terms),
+        out_specs=(vmem, vmem),
+        compiler_params=pltpu.CompilerParams(vmem_limit_bytes=4 * 2**20),
+        name="finish",
+    )(*in_vmem(*terms))
 
 
 def move_sums(
@@ -369,28 +466,21 @@
     owners,
 ):
     steps_count, row_count, heads_here, head_size = queries.shape
-    replicas, tensors = lax.axis_size("replica"), lax.axis_size("tensor")
     model = out_weight.shape[2]
-    share = replicas * row_count // tensors
-    lines = steps_count * share
     split = attend_split(queries, cache_keys, cache_values, new_keys, new_values, lengths)
     gathered = lax.all_to_all(split, "replica", split_axis=0, concat_axis=0, tiled=True)
     gathered = gathered.reshape(-1, gathered.shape[2])
-    rows, base_rows = select_rows(owners, finished, steps_count, row_count)
-    weight = out_weight.reshape(-1, model)
-    operands = (gathered, rows, base_rows, base_stream, weight)
+    weight = pltpu.with_memory_space_constraint(out_weight.reshape(-1, model), pltpu.HBM)
+    rows, base_rows, early, late = select_rows(owners, finished, weight, steps_count, row_count)
+    operands = (gathered, rows, base_rows, base_stream)
     core, across = ("tensor", 1), ("tensor", 2)
     beside, along = ("replica", 1), ("replica", 2)
-    total = jnp.concatenate(
-        [
-            reduce_scatter(*project(0, *operands), (core, across, beside, along)),
-            reduce_scatter(*project(1, *operands), (core, beside, across, along)),
-        ],
-        axis=1,
-    )
-    updates = total[:lines].reshape(steps_count, share, model // replicas)
-    trainer_rows = total[lines:].reshape(1, SLOT_DEV, model)
-    return (updates, trainer_rows)
+    second = first_stages(*project(1, *operands, early, weight), (core, beside, across))
+    first = first_stages(*project(0, *operands, late, weight), (core, across, beside))
+    own, *sends = join(first, second)
+    came = [exchange(v, along[0], along[1] * (m + 1)) for m, v in enumerate(sends)]
+    updates, trainer_rows = finish(steps_count, (own, *came))
+    return (updates, trainer_rows.reshape(1, SLOT_DEV, model))
 
 
 def shards(*arrays):

time: 60 us -> 51.1 us (0.85)
  local copies, waits for them, and re-layouts: 9.49 us -> 0.01 us
  Pallas kernels: 6.72 us -> 11.9 us
  starting transfers between devices: 19.1 us -> 16.4 us
  waiting for transfers between devices: 22.3 us -> 21.4 us
  other arithmetic: 1.24 us -> 0.37 us
    unnamed x20 -> x6, local copies, waits for them, and re-layouts: 8.86 us -> 0.01 us
    ppermute x12 -> x9, starting transfers between devices: 11.8 us -> 9.1 us  [exchange(): return lax.ppermute(value, axis, [(i, i ^ mask) for i in range(size)])]
    all_to_all x1, waiting for transfers between devices: 6.16 us -> 4.31 us  [move_sums(): lax.all_to_all(split, 'replica', split_axis=0, concat_axis=0, tiled=True)]
    pallas_call x1, Pallas kernels: 0.66 us -> 2.5 us  [select_rows(): pl.pallas_call(functools.partial(select_kernel, (tensors, replicas, steps...]
    pallas_call x2, Pallas kernels: 1.37 us -> 2.84 us  [project(): pl.pallas_call(functools.partial(project_kernel, (tensors, replicas, tall...]
    pallas_call x1, Pallas kernels: 4.69 us -> 5.74 us  [attend_split(): pl.pallas_call(functools.partial(attend_kernel, 1.0 / math.sqrt(head_size...]
    ppermute x12 -> x9, waiting for transfers between devices: 16.1 us -> 17.1 us  [exchange(): return lax.ppermute(value, axis, [(i, i ^ mask) for i in range(size)])]
    pallas_call x0 -> x2, Pallas kernels: none -> 0.83 us  [the longest x1 0.67 us: finish(): pl.pallas_call(finish_kernel, out_shape=(jax.ShapeDtypeStruct((steps_coun...]
  transfers between devices with their start and end apart: 13 -> 10, of which waited for: 8 -> 8; matrix products, arithmetic and copies ran while one was open for 1% -> 1% of each run, Pallas kernels for 2% -> 9%
where the time goes in v3:
time: 51.1 us; the launch traced here: 50.9 us
  waiting for transfers between devices  21.4 us (42%)
  starting transfers between devices  16.4 us (32%)
  Pallas kernels  11.9 us (23%)
  between operations  0.72 us (1%)
    ppermute x9, waiting for transfers between devices, exchange(): return lax.ppermute(value, axis, [(i, i ^ mask) for i in range(size)])  17.1 us
    ppermute x9, starting transfers between devices, exchange(): return lax.ppermute(value, axis, [(i, i ^ mask) for i in range(size)])  9.1 us
    all_to_all x1, starting transfers between devices, move_sums(): lax.all_to_all(split, 'replica', split_axis=0, concat_axis=0, tiled=True)  7.32 us
    pallas_call x1, Pallas kernels, attend_split(): pl.pallas_call(functools.partial(attend_kernel, 1.0 / math.sqrt(head_size...  5.74 us
    all_to_all x1, waiting for transfers between devices, move_sums(): lax.all_to_all(split, 'replica', split_axis=0, concat_axis=0, tiled=True)  4.31 us
    pallas_call x2, Pallas kernels, project(): pl.pallas_call(functools.partial(project_kernel, (tensors, replicas, tall...  2.84 us
    pallas_call x1, Pallas kernels, select_rows(): pl.pallas_call(functools.partial(select_kernel, (tensors, replicas, steps...  2.5 us
  transfers between devices with their start and end apart: 10, of which 8 were waited for; matrix products, arithmetic and copies ran while one was open for 1% of the time, Pallas kernels for 9%

profile of v3, /device:TPU:0, one launch (start us, length us, event | category | flops | bytes accessed | tf_op | source)
XLA Modules:
  0.0 50.9 jit_solution(6022621287671666)
XLA Ops:
  0.6 0.0 copy-start.1
  0.6 0.0 copy-start.2
  0.7 5.7 %attend.1 = bf16[128,256]{1,0:T(8,128)(2,1)} custom-call(s32[4]{0:T(128)} %refs_0_.1, bf16[4,4,16,128]{3,2,1,0:T(8,128)(2,1)} %refs_1_.1, bf16[4,4,2,128]{3,2,1,0:T(2,128)(2,1)} %refs_2_.1, bf16[4,4,2,128]{3,2,1,0:T(2,128)(2,1)} %refs_3_.3, bf16[4,2,1536,128]{3,2,1,0:T(8,128)(2,1)} %refs_4_.1, bf16[4,2,1536,128]{3,2,1,0:T(8,128)(2,1)} %refs_5_.1), custom_call_target="tpu_custom_call" | custom-call | flops 201326592 | bytes 6291456 | tf_op jit(solution)/shard_map/attend/pallas_call | solution.py:193
  6.4 0.0 copy-start
  6.4 7.3 %all-to-all-start = ((bf16[8,16,256]{2,1,0:T(8,128)(2,1)}), bf16[8,16,256]{2,1,0:T(8,128)(2,1)S(1)}, u32[]{:S(2)}, u32[]{:S(2)}) async-start(bf16[8,16,256]{2,1,0:T(8,128)(2,1)} %bitcast.2), calls=%async_computation | async-start | bytes 131072 | tf_op jit(solution)/shard_map/all_to_all | solution.py:471
  13.7 0.1 pad_add_fusion.me
  13.8 0.0 copy-done.1
  13.8 0.0 copy-done.2
  13.8 2.5 %select.1 = (bf16[160,128]{1,0:T(8,128)(2,1)S(1)}, bf16[32,8]{1,0:T(8,128)(2,1)S(1)}, bf16[256,4096]{1,0:T(8,128)(2,1)S(1)}, bf16[256,2048]{1,0:T(8,128)(2,1)S(1)}) custom-call(s32[2]{0:T(128)S(1)} %pad_add_fusion.me, s32[32]{0:T(128)S(1)} %bitcast.27, s32[32]{0:T(128)S(1)} %copy-done.2, bf16[256,8192]{1,0:T(8,128)(2,1)} %bitcast.28), custom_call_target="tpu_custom_call" | custom-call | flops 1000000 | bytes 4194304 | tf_op jit(solution)/shard_map/select/pallas_call | solution.py:286
  16.3 4.3 %all-to-all-done = bf16[8,16,256]{2,1,0:T(8,128)(2,1)S(1)} async-done(((bf16[8,16,256]{2,1,0:T(8,128)(2,1)}), bf16[8,16,256]{2,1,0:T(8,128)(2,1)S(1)}, u32[]{:S(2)}, u32[]{:S(2)}) %all-to-all-start) | async-done | bytes 65568 | tf_op jit(solution)/shard_map/all_to_all | solution.py:471
  20.6 0.0 copy-done
  20.6 0.7 %project_1.1 = (bf16[2,2,4,40,512]{4,3,2,1,0:T(8,128)(2,1)S(1)}, bf16[2,2,4,40,512]{4,3,2,1,0:T(8,128)(2,1)S(1)}) custom-call(s32[1]{0:T(128)} %bitcast.me_ref, bf16[256,8192]{1,0:T(8,128)(2,1)} %bitcast.29, bf16[128,256]{1,0:T(8,128)(2,1)S(1)} %bitcast.25, bf16[160,128]{1,0:T(8,128)(2,1)S(1)} %get-tuple-element.16.refs_1_, ...), custom_call_target="tpu_custom_call" | custom-call | flops 335544320 | bytes 2097152 | tf_op jit(solution)/shard_map/project_1/pallas_call | solution.py:364
  21.3 0.1 collective-permute-start.3
  21.4 2.1 %project_0.1 = (bf16[2,2,4,40,512]{4,3,2,1,0:T(8,128)(2,1)S(1)}, bf16[2,2,4,40,512]{4,3,2,1,0:T(8,128)(2,1)S(1)}) custom-call(s32[1]{0:T(128)} %bitcast.me_ref, bf16[256,8192]{1,0:T(8,128)(2,1)} %bitcast.30, bf16[128,256]{1,0:T(8,128)(2,1)S(1)} %bitcast.26, bf16[160,128]{1,0:T(8,128)(2,1)S(1)} %get-tuple-element.16.refs_1_, ...), custom_call_target="tpu_custom_call" | custom-call | flops 335544320 | bytes 2097152 | tf_op jit(solution)/shard_map/project_0/pallas_call | solution.py:364
  23.6 0.6 %collective-permute-start = (bf16[2,2,4,40,512]{4,3,2,1,0:T(8,128)(2,1)S(1)}, bf16[2,2,4,40,512]{4,3,2,1,0:T(8,128)(2,1)S(1)}, u32[]{:S(2)}, u32[]{:S(2)}) collective-permute-start(bf16[2,2,4,40,512]{4,3,2,1,0:T(8,128)(2,1)S(1)} %get-tuple-element.20), channel_id=1, source_target_pairs={{0,1},{1,0},{2,3},{3,2},{4,5},{5,4},{6,7},{7,6},{8,9},{9,8},{10,11... | collective-permute-start | bytes 1966088 | tf_op jit(solution)/shard_map/ppermute | solution.py:386
  24.1 0.0 collective-permute-done.3.refs_5_
  24.1 0.1 fusion.1
  24.2 0.5 collective-permute-start.4
  24.7 1.2 %collective-permute-done.refs_1_ = bf16[2,2,4,40,512]{4,3,2,1,0:T(8,128)(2,1)S(1)} collective-permute-done((bf16[2,2,4,40,512]{4,3,2,1,0:T(8,128)(2,1)S(1)}, bf16[2,2,4,40,512]{4,3,2,1,0:T(8,128)(2,1)S(1)}, u32[]{:S(2)}, u32[]{:S(2)}) %collective-permute-start) | collective-permute-done | bytes 655392 | tf_op jit(solution)/shard_map/ppermute | solution.py:386
  25.9 0.1 fusion
  25.9 1.6 %collective-permute-start.1 = (bf16[2,4,40,512]{3,2,1,0:T(8,128)(2,1)S(1)}, bf16[2,4,40,512]{3,2,1,0:T(8,128)(2,1)S(1)}, u32[]{:S(2)}, u32[]{:S(2)}) collective-permute-start(bf16[2,4,40,512]{3,2,1,0:T(8,128)(2,1)S(1)} %fusion), channel_id=1, source_target_pairs={{0,2},{1,3},{2,0},{3,1},{4,6},{5,7},{6,4},{7,5},{8,10},{9,11},{10,... | collective-permute-start | bytes 983048 | tf_op jit(solution)/shard_map/ppermute | solution.py:386
  27.5 6.4 %collective-permute-done.4.refs_6_ = bf16[2,4,40,512]{3,2,1,0:T(8,128)(2,1)S(1)} collective-permute-done((bf16[2,4,40,512]{3,2,1,0:T(8,128)(2,1)S(1)}, bf16[2,4,40,512]{3,2,1,0:T(8,128)(2,1)S(1)}, u32[]{:S(2)}, u32[]{:S(2)}) %collective-permute-start.4) | collective-permute-done | bytes 327712 | tf_op jit(solution)/shard_map/ppermute | solution.py:386
  33.9 0.1 fusion.2
  34.0 1.6 %collective-permute-start.5 = (bf16[4,40,512]{2,1,0:T(8,128)(2,1)S(1)}, bf16[4,40,512]{2,1,0:T(8,128)(2,1)S(1)}, u32[]{:S(2)}, u32[]{:S(2)}) collective-permute-start(bf16[4,40,512]{2,1,0:T(8,128)(2,1)S(1)} %fusion.2), channel_id=1, source_target_pairs={{0,2},{1,3},{2,0},{3,1},{4,6},{5,7},{6,4},{7,5},{8,10},{9,11},{10,... | collective-permute-start | bytes 491528 | tf_op jit(solution)/shard_map/ppermute | solution.py:386
  35.5 0.6 %collective-permute-done.1.refs_2_ = bf16[2,4,40,512]{3,2,1,0:T(8,128)(2,1)S(1)} collective-permute-done((bf16[2,4,40,512]{3,2,1,0:T(8,128)(2,1)S(1)}, bf16[2,4,40,512]{3,2,1,0:T(8,128)(2,1)S(1)}, u32[]{:S(2)}, u32[]{:S(2)}) %collective-permute-start.1) | collective-permute-done | bytes 327712 | tf_op jit(solution)/shard_map/ppermute | solution.py:386
  36.2 0.1 fusion.3
  36.2 0.5 collective-permute-start.2
  36.7 2.8 %collective-permute-done.5.refs_7_ = bf16[4,40,512]{2,1,0:T(8,128)(2,1)S(1)} collective-permute-done((bf16[4,40,512]{2,1,0:T(8,128)(2,1)S(1)}, bf16[4,40,512]{2,1,0:T(8,128)(2,1)S(1)}, u32[]{:S(2)}, u32[]{:S(2)}) %collective-permute-start.5) | collective-permute-done | bytes 163872 | tf_op jit(solution)/shard_map/ppermute | solution.py:386
  39.5 2.2 %collective-permute-done.2.refs_3_ = bf16[4,40,512]{2,1,0:T(8,128)(2,1)S(1)} collective-permute-done((bf16[4,40,512]{2,1,0:T(8,128)(2,1)S(1)}, bf16[4,40,512]{2,1,0:T(8,128)(2,1)S(1)}, u32[]{:S(2)}, u32[]{:S(2)}) %collective-permute-start.2) | collective-permute-done | bytes 163872 | tf_op jit(solution)/shard_map/ppermute | solution.py:386
  41.8 0.2 join.1
  41.9 0.3 collective-permute-start.6
  42.2 0.9 %collective-permute-start.7 = (bf16[40,1024]{1,0:T(8,128)(2,1)S(1)}, bf16[40,1024]{1,0:T(8,128)(2,1)S(1)}, u32[]{:S(2)}, u32[]{:S(2)}) collective-permute-start(bf16[40,1024]{1,0:T(8,128)(2,1)S(1)} %get-tuple-element.26), channel_id=1, source_target_pairs={{0,16},{4,20},{8,24},{12,28},{16,0},{20,4},{24,8},{28,12},{1,17},{... | collective-permute-start | bytes 245768 | tf_op jit(solution)/shard_map/ppermute | solution.py:386
  43.1 3.3 %collective-permute-start.8 = (bf16[40,1024]{1,0:T(8,128)(2,1)S(1)}, bf16[40,1024]{1,0:T(8,128)(2,1)S(1)}, u32[]{:S(2)}, u32[]{:S(2)}) collective-permute-start(bf16[40,1024]{1,0:T(8,128)(2,1)S(1)} %get-tuple-element.27), channel_id=1, source_target_pairs={{0,24},{4,28},{8,16},{12,20},{16,8},{20,12},{24,0},{28,4},{1,25},{... | collective-permute-start | bytes 245768 | tf_op jit(solution)/shard_map/ppermute | solution.py:386
  46.4 0.1 collective-permute-done.6.refs_1_
  46.4 3.8 %collective-permute-done.7.refs_2_ = bf16[40,1024]{1,0:T(8,128)(2,1)S(1)} collective-permute-done((bf16[40,1024]{1,0:T(8,128)(2,1)S(1)}, bf16[40,1024]{1,0:T(8,128)(2,1)S(1)}, u32[]{:S(2)}, u32[]{:S(2)}) %collective-permute-start.7) | collective-permute-done | bytes 81952 | tf_op jit(solution)/shard_map/ppermute | solution.py:386
  50.2 0.0 collective-permute-done.8.refs_3_
  50.2 0.7 %finish.1 = (bf16[4,8,1024]{2,1,0:T(8,128)(2,1)}, bf16[1,8192]{1,0:T(2,128)(2,1)}) custom-call(f32[40,1024]{1,0:T(8,128)S(1)} %get-tuple-element.24.refs_0_, bf16[40,1024]{1,0:T(8,128)(2,1)S(1)} %collective-permute-done.6.refs_1_, bf16[40,1024]{1,0:T(8,128)(2,1)S(1)} %collective-permute-done.7.refs_2_, bf16[40,1024]{1,0:T(8,128)(2,1)S(1)} %collective-permute-done.8.refs_3_), custom_call_target="tpu_custom_call" | custom-call | tf_op jit(solution)/shard_map/finish/pallas_call | solution.py:443
Async XLA Ops:
  0.6 13.2 %copy-start.1 = (s32[32,1]{0,1:T(1,128)S(1)}, s32[32,1]{0,1:T(1,128)}, u32[]{:S(2)}) copy-start(s32[32,1]{0,1:T(1,128)} %param.19) | copy-start | bytes 388
  0.6 13.2 %copy-start.2 = (s32[32]{0:T(128)S(1)}, s32[32]{0:T(128)}, u32[]{:S(2)}) copy-start(s32[32]{0:T(128)} %finished.1) | copy-start | bytes 388
  6.4 14.2 %copy-start = (bf16[8,1024]{1,0:T(8,128)(2,1)S(1)}, bf16[8,1024]{1,0:T(8,128)(2,1)}, u32[]{:S(2)}) copy-start(bf16[8,1024]{1,0:T(8,128)(2,1)} %refs_3_.5) | copy-start | bytes 49156
  6.4 14.2 %all-to-all-start = ((bf16[8,16,256]{2,1,0:T(8,128)(2,1)}), bf16[8,16,256]{2,1,0:T(8,128)(2,1)S(1)}, u32[]{:S(2)}, u32[]{:S(2)}) async-start(bf16[8,16,256]{2,1,0:T(8,128)(2,1)} %bitcast.2), calls=%async_computation | async-start | bytes 131072 | tf_op jit(solution)/shard_map/all_to_all | solution.py:471
  21.3 2.8 %collective-permute-start.3 = (bf16[2,2,4,40,512]{4,3,2,1,0:T(8,128)(2,1)S(1)}, bf16[2,2,4,40,512]{4,3,2,1,0:T(8,128)(2,1)S(1)}, u32[]{:S(2)}, u32[]{:S(2)}) collective-permute-start(bf16[2,2,4,40,512]{4,3,2,1,0:T(8,128)(2,1)S(1)} %get-tuple-element.23), channel_id=1, source_target_pairs={{0,1},{1,0},{2,3},{3,2},{4,5},{5,4},{6,7},{7,6},{8,9},{9,8},{10,11... | collective-permute-start | bytes 1966088 | tf_op jit(solution)/shard_map/ppermute | solution.py:386
  23.6 2.3 %collective-permute-start = (bf16[2,2,4,40,512]{4,3,2,1,0:T(8,128)(2,1)S(1)}, bf16[2,2,4,40,512]{4,3,2,1,0:T(8,128)(2,1)S(1)}, u32[]{:S(2)}, u32[]{:S(2)}) collective-permute-start(bf16[2,2,4,40,512]{4,3,2,1,0:T(8,128)(2,1)S(1)} %get-tuple-element.20), channel_id=1, source_target_pairs={{0,1},{1,0},{2,3},{3,2},{4,5},{5,4},{6,7},{7,6},{8,9},{9,8},{10,11... | collective-permute-start | bytes 1966088 | tf_op jit(solution)/shard_map/ppermute | solution.py:386
  24.2 9.7 %collective-permute-start.4 = (bf16[2,4,40,512]{3,2,1,0:T(8,128)(2,1)S(1)}, bf16[2,4,40,512]{3,2,1,0:T(8,128)(2,1)S(1)}, u32[]{:S(2)}, u32[]{:S(2)}) collective-permute-start(bf16[2,4,40,512]{3,2,1,0:T(8,128)(2,1)S(1)} %fusion.1), channel_id=1, source_target_pairs={{0,4},{4,0},{8,12},{12,8},{16,20},{20,16},{24,28},{28,24},{1,5},{5... | collective-permute-start | bytes 983048 | tf_op jit(solution)/shard_map/ppermute | solution.py:386
  25.9 10.2 %collective-permute-start.1 = (bf16[2,4,40,512]{3,2,1,0:T(8,128)(2,1)S(1)}, bf16[2,4,40,512]{3,2,1,0:T(8,128)(2,1)S(1)}, u32[]{:S(2)}, u32[]{:S(2)}) collective-permute-start(bf16[2,4,40,512]{3,2,1,0:T(8,128)(2,1)S(1)} %fusion), channel_id=1, source_target_pairs={{0,2},{1,3},{2,0},{3,1},{4,6},{5,7},{6,4},{7,5},{8,10},{9,11},{10,... | collective-permute-start | bytes 983048 | tf_op jit(solution)/shard_map/ppermute | solution.py:386
  34.0 5.5 %collective-permute-start.5 = (bf16[4,40,512]{2,1,0:T(8,128)(2,1)S(1)}, bf16[4,40,512]{2,1,0:T(8,128)(2,1)S(1)}, u32[]{:S(2)}, u32[]{:S(2)}) collective-permute-start(bf16[4,40,512]{2,1,0:T(8,128)(2,1)S(1)} %fusion.2), channel_id=1, source_target_pairs={{0,2},{1,3},{2,0},{3,1},{4,6},{5,7},{6,4},{7,5},{8,10},{9,11},{10,... | collective-permute-start | bytes 491528 | tf_op jit(solution)/shard_map/ppermute | solution.py:386
  36.2 5.5 %collective-permute-start.2 = (bf16[4,40,512]{2,1,0:T(8,128)(2,1)S(1)}, bf16[4,40,512]{2,1,0:T(8,128)(2,1)S(1)}, u32[]{:S(2)}, u32[]{:S(2)}) collective-permute-start(bf16[4,40,512]{2,1,0:T(8,128)(2,1)S(1)} %fusion.3), channel_id=1, source_target_pairs={{0,4},{4,0},{8,12},{12,8},{16,20},{20,16},{24,28},{28,24},{1,5},{5... | collective-permute-start | bytes 491528 | tf_op jit(solution)/shard_map/ppermute | solution.py:386
  41.9 4.5 %collective-permute-start.6 = (bf16[40,1024]{1,0:T(8,128)(2,1)S(1)}, bf16[40,1024]{1,0:T(8,128)(2,1)S(1)}, u32[]{:S(2)}, u32[]{:S(2)}) collective-permute-start(bf16[40,1024]{1,0:T(8,128)(2,1)S(1)} %get-tuple-element.25), channel_id=1, source_target_pairs={{0,8},{4,12},{8,0},{12,4},{16,24},{20,28},{24,16},{28,20},{1,9},{5... | collective-permute-start | bytes 245768 | tf_op jit(solution)/shard_map/ppermute | solution.py:386
  42.2 8.0 %collective-permute-start.7 = (bf16[40,1024]{1,0:T(8,128)(2,1)S(1)}, bf16[40,1024]{1,0:T(8,128)(2,1)S(1)}, u32[]{:S(2)}, u32[]{:S(2)}) collective-permute-start(bf16[40,1024]{1,0:T(8,128)(2,1)S(1)} %get-tuple-element.26), channel_id=1, source_target_pairs={{0,16},{4,20},{8,24},{12,28},{16,0},{20,4},{24,8},{28,12},{1,17},{... | collective-permute-start | bytes 245768 | tf_op jit(solution)/shard_map/ppermute | solution.py:386
  43.1 7.1 %collective-permute-start.8 = (bf16[40,1024]{1,0:T(8,128)(2,1)S(1)}, bf16[40,1024]{1,0:T(8,128)(2,1)S(1)}, u32[]{:S(2)}, u32[]{:S(2)}) collective-permute-start(bf16[40,1024]{1,0:T(8,128)(2,1)S(1)} %get-tuple-element.27), channel_id=1, source_target_pairs={{0,24},{4,28},{8,16},{12,20},{16,8},{20,12},{24,0},{28,4},{1,25},{... | collective-permute-start | bytes 245768 | tf_op jit(solution)/shard_map/ppermute | solution.py:386

commit v4 on v3

--- a/solution.py
+++ b/solution.py
@@ -8,8 +8,10 @@
 from jax.experimental.pallas import tpu as pltpu
 from jax.sharding import PartitionSpec as P
 
+
 SLOT_DEV = 1
 LANES = 128
+EARLY = (8, 5)
 
 
 def attend(queries, cache_keys, cache_values, new_keys, new_values, lengths):
@@ -106,7 +108,7 @@
     return (updates, trainer_rows)
 
 
-def attend_kernel(scale, *refs):
+def attend_kernel(factor, *refs):
     sources, out, places, (fresh_k, fresh_v, turned, sems) = refs[:6], refs[6], refs[7:13], refs[13:]
     lengths, queries, new_keys, new_values, keys, held = places
     steps_count, row_count, heads_here, head_size = queries.shape
@@ -132,42 +134,48 @@
     fresh_at = lax.broadcasted_iota(jnp.int32, (lines, LANES), 1)
     fresh_step = lax.broadcasted_iota(jnp.int32, (lines, LANES), 0) // group
     fresh_valid = fresh_at <= fresh_step
+    low = f32(-1e30)
     width = head_size // group
     lane = lax.broadcasted_iota(jnp.int32, (group, head_size), 1) // width
     diagonal = (lane - lax.broadcasted_iota(jnp.int32, (group, head_size), 0)) & (group - 1)
     turn = (((1,), (1,)), ((), ()))
-    for copy in small:
-        copy.wait()
-    for i in range(row_count):
-        fetches[i][0].wait()
+
+    def fresh_parts(i):
+        for g in range(kv_here):
+            for t in range(steps_count):
+                fresh_k[i, g, t : t + 1] = new_keys[t, i, g : g + 1]
+                fresh_v[i, g, t : t + 1] = new_values[t, i, g : g + 1]
+
+    def score(i):
         is_valid = place < lengths[i]
-        weighed = []
+        found = []
         for g in range(kv_here):
             query = jnp.concatenate(
                 [queries[t, i, g * group : (g + 1) * group] for t in range(steps_count)], axis=0
             )
-            for t in range(steps_count):
-                fresh_k[g, t : t + 1] = new_keys[t, i, g : g + 1]
-                fresh_v[g, t : t + 1] = new_values[t, i, g : g + 1]
-            scores = lax.dot_general(query, keys[i, g], turn, preferred_element_type=f32) * scale
-            scores = jnp.where(is_valid, scores, f32(-1e30))
-            fresh = lax.dot_general(query, fresh_k[g], turn, preferred_element_type=f32) * scale
-            fresh = jnp.where(fresh_valid, fresh, f32(-1e30))
+            scores = lax.dot_general(query, keys[i, g], turn, preferred_element_type=f32)
+            fresh = lax.dot_general(query, fresh_k[i, g], turn, preferred_element_type=f32)
+            found.append((jnp.where(is_valid, scores, low), jnp.where(fresh_valid, fresh, low)))
+        return found
+
+    def weigh(found):
+        weighed = []
+        for scores, fresh in found:
             highest = jnp.maximum(
                 jnp.max(scores, axis=1, keepdims=True), jnp.max(fresh, axis=1, keepdims=True)
             )
-            scores = jnp.exp(scores - highest)
-            fresh = jnp.exp(fresh - highest)
+            scores = jnp.exp2((scores - highest) * factor)
+            fresh = jnp.exp2((fresh - highest) * factor)
             total = jnp.sum(scores, axis=1, keepdims=True) + jnp.sum(fresh, axis=1, keepdims=True)
-            share = 1.0 / total
-            weighed.append(
-                ((scores * share).astype(jnp.bfloat16), (fresh * share).astype(jnp.bfloat16))
-            )
-        fetches[i][1].wait()
+            weighed.append((scores.astype(jnp.bfloat16), fresh.astype(jnp.bfloat16), 1.0 / total))
+        return weighed
+
+    def mix(i, weighed):
         for g in range(kv_here):
-            probs, fresh_probs = weighed[g]
-            mixed = jnp.dot(probs, held[i, g], preferred_element_type=f32)
-            mixed = mixed + jnp.dot(fresh_probs, fresh_v[g], preferred_element_type=f32)
+            weights, fresh_weights, share = weighed[g]
+            mixed = jnp.dot(weights, held[i, g], preferred_element_type=f32)
+            mixed = mixed + jnp.dot(fresh_weights, fresh_v[i, g], preferred_element_type=f32)
+            mixed = mixed * share
             for t in range(steps_count):
                 part = mixed[t * group : (t + 1) * group]
                 moved = jnp.where(diagonal == 0, part, 0.0)
@@ -175,12 +183,35 @@
                     rolled = pltpu.roll(pltpu.roll(part, group - d, 0), d * width, 1)
                     moved = jnp.where(diagonal == d, rolled, moved)
                 turned[g, pl.ds(t * row_count + i, group, stride=steps_count * row_count), :] = moved
+
+    for copy in small:
+        copy.wait()
+    for i in range(row_count):
+        fresh_parts(i)
+    fetches[0][0].wait()
+    found = score(0)
+    for i in range(row_count):
+        later = None
+        if i + 1 < row_count:
+            fetches[i][1].wait()
+            fetches[i + 1][0].wait()
+            later = score(i + 1)
+        else:
+            fetches[i][1].wait()
+        mix(i, weigh(found))
+        found = later
     for g in range(kv_here):
-        out[:, g * head_size : (g + 1) * head_size] = turned[g].astype(jnp.bfloat16)
+        out[:, :, g * head_size : (g + 1) * head_size] = (
+            turned[g].reshape(out.shape[:2] + (head_size,)).astype(jnp.bfloat16)
+        )
 
 
 def in_vmem(*arrays):
     return [pltpu.with_memory_space_constraint(v, pltpu.VMEM) for v in arrays]
+
+
+def in_hbm(*arrays):
+    return [pltpu.with_memory_space_constraint(v, pltpu.HBM) for v in arrays]
 
 
 def attend_split(queries, cache_keys, cache_values, new_keys, new_values, lengths):
@@ -191,15 +222,15 @@
     operands = (lengths, queries, new_keys, new_values, cache_keys, cache_values)
     vmem = pl.BlockSpec(memory_space=pltpu.VMEM)
     (out,) = pl.pallas_call(
-        functools.partial(attend_kernel, 1.0 / math.sqrt(head_size)),
-        out_shape=(pltpu.VMEM((group * lines, kv_here * head_size), jnp.bfloat16),),
+        functools.partial(attend_kernel, math.log2(math.e) / math.sqrt(head_size)),
+        out_shape=(pltpu.VMEM((group, lines, kv_here * head_size), jnp.bfloat16),),
         in_specs=[pl.BlockSpec(memory_space=pltpu.HBM)] * len(operands),
         out_specs=(vmem,),
         scratch_shapes=[
             pltpu.SMEM(lengths.shape, lengths.dtype),
             *(pltpu.VMEM(v.shape, v.dtype) for v in operands[1:]),
-            pltpu.VMEM((kv_here, LANES, head_size), jnp.bfloat16),
-            pltpu.VMEM((kv_here, LANES, head_size), jnp.bfloat16),
+            pltpu.VMEM((row_count, kv_here, LANES, head_size), jnp.bfloat16),
+            pltpu.VMEM((row_count, kv_here, LANES, head_size), jnp.bfloat16),
             pltpu.VMEM((kv_here, group * lines, head_size), jnp.float32),
             pltpu.SemaphoreType.DMA((4 + 2 * row_count,)),
         ],
@@ -210,35 +241,42 @@
             transcendentals=lines * heads_here * positions_count,
         ),
         name="attend",
-    )(*[pltpu.with_memory_space_constraint(v, pltpu.HBM) for v in operands])
-    return out.reshape(group, lines, kv_here * head_size)
-
-
-def fetch_weight(weight, held, sems, me, part, blocks):
-    if not blocks:
-        return []
-    half = held.shape[1] // len(blocks)
+    )(*in_hbm(*operands))
+    return out
+
+
+def fetch_weight(weight, held, sems, columns, blocks):
+    start, width = columns
+    block = weight.shape[1] // lax.axis_size("replica")
+    me = lax.axis_index("replica")
     return [
         pltpu.make_async_copy(
-            weight.at[:, pl.ds(pl.multiple_of(((r ^ me) * 2 + part) * half, half), half)],
-            held.at[:, pl.ds(n * half, half)],
+            weight.at[:, pl.ds(pl.multiple_of((r ^ me) * block + start, LANES), width)],
+            held.at[:, pl.ds(n * width, width)],
             sems.at[n],
         )
         for n, r in enumerate(blocks)
     ]
 
 
-def select_kernel(sizes, me, owners, finished, weight, rows, base_rows, early, late, *sems):
+def select_kernel(sizes, calls, owners_at, finished_at, weight, rows, base_rows, *refs):
     tensors, replicas, steps_count, row_count = sizes
+    held, (owners, finished, small), sems = refs[: len(calls)], refs[len(calls) :][:3], refs[len(calls) + 3 :]
     total_rows = replicas * row_count
     share = total_rows // tensors
     lines = steps_count * share
-    me_r, me_t = me[0], me[1]
-    blocks = range(replicas)
-    fetches = fetch_weight(weight, early, sems[0], me_r, 1, blocks)
-    fetches += fetch_weight(weight, late, sems[1], me_r, 0, blocks[: replicas // 2])
-    for fetch in fetches:
+    me_r, me_t = lax.axis_index("replica"), lax.axis_index("tensor")
+    first = [
+        pltpu.make_async_copy(owners_at, owners, small.at[0]),
+        pltpu.make_async_copy(finished_at, finished, small.at[1]),
+    ]
+    fetches = []
+    for columns, ref, sem in zip(calls, held, sems):
+        fetches += fetch_weight(weight, ref, sem, columns, range(ref.shape[1] // columns[1]))
+    for fetch in first + fetches:
         fetch.start()
+    for fetch in first:
+        fetch.wait()
 
     def tell(row_of):
         name, rank, done = (jnp.zeros_like(row_of) for _ in range(3))
@@ -276,109 +314,127 @@
         fetch.wait()
 
 
-def select_rows(owners, finished, weight, steps_count, row_count):
+def select_rows(owners, finished, weight, calls, early, steps_count, row_count):
     replicas, tensors = lax.axis_size("replica"), lax.axis_size("tensor")
-    me = jnp.stack([lax.axis_index("replica"), lax.axis_index("tensor")]).astype(jnp.int32)
     share = replicas * row_count // tensors
-    smem, vmem = pl.BlockSpec(memory_space=pltpu.SMEM), pl.BlockSpec(memory_space=pltpu.VMEM)
+    hbm, vmem = pl.BlockSpec(memory_space=pltpu.HBM), pl.BlockSpec(memory_space=pltpu.VMEM)
     height = tensors * (steps_count * share + replicas)
-    depth, model = weight.shape
+    names = owners[:, 0]
     return pl.pallas_call(
-        functools.partial(select_kernel, (tensors, replicas, steps_count, row_count)),
+        functools.partial(select_kernel, (tensors, replicas, steps_count, row_count), calls),
         out_shape=(
             pltpu.VMEM((height, steps_count * replicas * row_count), jnp.bfloat16),
             pltpu.VMEM((tensors * replicas, share), jnp.bfloat16),
-            pltpu.VMEM((depth, model // 2), weight.dtype),
-            pltpu.VMEM((depth, model // 4), weight.dtype),
+            *(
+                pltpu.VMEM((weight.shape[0], blocks * width), weight.dtype)
+                for blocks, (_, width) in zip(early, calls)
+            ),
         ),
-        in_specs=[smem, smem, smem, pl.BlockSpec(memory_space=pltpu.HBM)],
-        out_specs=[vmem] * 4,
+        in_specs=[hbm] * 3,
+        out_specs=[vmem] * (2 + len(calls)),
         scratch_shapes=[
-            pltpu.SemaphoreType.DMA((replicas,)),
-            pltpu.SemaphoreType.DMA((replicas // 2,)),
+            pltpu.SMEM(names.shape, names.dtype),
+            pltpu.SMEM(finished.shape, finished.dtype),
+            pltpu.SemaphoreType.DMA((2,)),
+            *(pltpu.SemaphoreType.DMA((blocks,)) for blocks in early),
         ],
         compiler_params=pltpu.CompilerParams(vmem_limit_bytes=4 * 2**20),
         cost_estimate=pl.CostEstimate(
             flops=10**6, bytes_accessed=2 * weight.size, transcendentals=0
         ),
         name="select",
-    )(me, owners[:, 0], finished, weight)
-
-
-def project_kernel(sizes, part, me_ref, weight, *refs):
-    gathered, rows, base_rows, base, first_weight, keep, send, slot_sums, rest, sems = refs
+    )(*in_hbm(names, finished, weight))
+
+
+def place(order, t, r):
+    tensors, replicas = lax.axis_size("tensor"), lax.axis_size("replica")
+    bits = {"x": (t // 2, tensors // 2), "y": (r % 2, 2), "z": (r // 2, replicas // 2)}
+    at = 0
+    for name in order:
+        at = at * bits[name][1] + bits[name][0]
+    return at
+
+
+def project_kernel(sizes, columns, order, later, *refs):
+    gathered, rows, base_rows, base, near, rest = refs[:6]
     tensors, replicas, lines = sizes
+    fetches = []
+    if later is None:
+        keep, send, slot_sums = refs[6:]
+    else:
+        keep, send, fetched, slot_sums, sems = refs[6:]
+        fetches = fetch_weight(rest, fetched, sems, later[0], range(later[1], replicas))
+    start, width = columns
     f32 = jnp.float32
-    me = me_ref[0]
-    half = keep.shape[-1]
-    near = first_weight.shape[1] // half
-    fetches = fetch_weight(weight, rest, sems, me, part, range(near, replicas))
+    me = lax.axis_index("replica")
+    tall = lines + replicas
+    found = near.shape[1] // width
     for fetch in fetches:
         fetch.start()
     held = jnp.dot(rows[...], gathered[...], preferred_element_type=f32).astype(jnp.bfloat16)
-    tall = lines + replicas
     extra = jnp.dot(
-        base_rows[...], base[:, part * half : (part + 1) * half], preferred_element_type=f32
-    )
-
-    def at(t, r):
-        ref = send if t % 2 else keep
-        return ref.at[(t // 2, r % 2, r // 2) if part == 0 else (r % 2, t // 2, r // 2)]
+        base_rows[...], base[:, start : start + width], preferred_element_type=f32
+    )
+
+    def target(t, r):
+        return (send if t % 2 else keep).at[place(order, t, r)]
 
     for r in range(replicas):
         block = r ^ me
-        if r < near:
-            columns = first_weight[:, r * half : (r + 1) * half]
+        if r < found:
+            own = near[:, r * width : (r + 1) * width]
         else:
-            fetches[r - near].wait()
-            columns = rest[:, (r - near) * half : (r - near + 1) * half]
-        sums = jnp.dot(held, columns, preferred_element_type=f32)
+            own = rest[:, (r - found) * width : (r - found + 1) * width]
+        sums = jnp.dot(held, own, preferred_element_type=f32)
         for t in range(tensors):
-            first = t * tall
-            at(t, r)[:lines] = sums[first : first + lines].astype(jnp.bfloat16)
-            slot = sums[first + lines : first + tall]
+            top = t * tall
+            target(t, r)[:lines] = sums[top : top + lines].astype(jnp.bfloat16)
+            slot = sums[top + lines : top + tall]
             if r == 0:
                 slot = slot + extra[t * replicas : (t + 1) * replicas]
-            for c in range(half // LANES):
+            for c in range(width // LANES):
                 slot_sums[t, c, pl.ds(block, replicas, stride=replicas), :] = slot[
                     :, c * LANES : (c + 1) * LANES
                 ]
     for t in range(tensors):
         for r in range(replicas):
-            for c in range(half // LANES):
-                at(t, r)[lines:, c * LANES : (c + 1) * LANES] = slot_sums[
+            for c in range(width // LANES):
+                target(t, r)[lines:, c * LANES : (c + 1) * LANES] = slot_sums[
                     t, c, r * replicas : (r + 1) * replicas
                 ].astype(jnp.bfloat16)
-
-
-def project(part, gathered, rows, base_rows, base_stream, first_weight, weight):
+    for fetch in fetches:
+        fetch.wait()
+
+
+def project(columns, order, later, gathered, rows, base_rows, base_stream, near, rest):
     replicas, tensors = lax.axis_size("replica"), lax.axis_size("tensor")
-    depth, model = weight.shape
-    half = model // replicas // 2
-    missing = max(1, replicas - first_weight.shape[1] // half)
+    depth = near.shape[0]
+    width = columns[1]
     tall = rows.shape[0] // tensors
-    me = lax.axis_index("replica").astype(jnp.int32).reshape(1)
-    lead = (tensors // 2, 2) if part == 0 else (2, tensors // 2)
-    shape = pltpu.VMEM(lead + (replicas // 2, tall, half), jnp.bfloat16)
-    smem, vmem = pl.BlockSpec(memory_space=pltpu.SMEM), pl.BlockSpec(memory_space=pltpu.VMEM)
+    shape = pltpu.VMEM((tensors // 2 * replicas, tall, width), jnp.bfloat16)
+    vmem = pl.BlockSpec(memory_space=pltpu.VMEM)
+    slot_sums = pltpu.VMEM((tensors, width // LANES, replicas * replicas, LANES), jnp.float32)
+    fetched, sems, space, constrain = (), (), pltpu.VMEM, in_vmem
+    if later is not None:
+        missing = replicas - later[1]
+        fetched = (pltpu.VMEM((depth, missing * later[0][1]), near.dtype),)
+        sems = (pltpu.SemaphoreType.DMA((missing,)),)
+        space, constrain = pltpu.HBM, in_hbm
     return pl.pallas_call(
-        functools.partial(project_kernel, (tensors, replicas, tall - replicas), part),
-        out_shape=(shape, shape),
-        in_specs=[smem, pl.BlockSpec(memory_space=pltpu.HBM)] + [vmem] * 5,
-        out_specs=(vmem, vmem),
-        scratch_shapes=[
-            pltpu.VMEM((tensors, half // LANES, replicas * replicas, LANES), jnp.float32),
-            pltpu.VMEM((depth, missing * half), weight.dtype),
-            pltpu.SemaphoreType.DMA((missing,)),
-        ],
+        functools.partial(
+            project_kernel, (tensors, replicas, tall - replicas), columns, order, later
+        ),
+        out_shape=(shape, shape, *fetched),
+        in_specs=[vmem] * 5 + [pl.BlockSpec(memory_space=space)],
+        out_specs=(vmem,) * (2 + len(fetched)),
+        scratch_shapes=[slot_sums, *sems],
         compiler_params=pltpu.CompilerParams(vmem_limit_bytes=8 * 2**20),
         cost_estimate=pl.CostEstimate(
-            flops=rows.shape[0] * depth * model,
-            bytes_accessed=depth * model,
+            flops=2 * rows.shape[0] * depth * width * replicas,
+            bytes_accessed=2 * depth * width * replicas,
             transcendentals=0,
         ),
-        name=f"project_{part}",
-    )(me, weight, *in_vmem(gathered, rows, base_rows, base_stream, first_weight))
+    )(*in_vmem(gathered, rows, base_rows, base_stream, near), *constrain(rest))
 
 
 def exchange(value, axis, mask):
@@ -390,34 +446,29 @@
     return functools.reduce(jnp.add, [v.astype(jnp.float32) for v in terms])
 
 
-def part_of(keep, came, *at):
-    return add_up([keep[at]] + [v[at[i:]] for i, v in enumerate(came)])
-
-
-def first_stages(keep, send, stages):
-    came = [exchange(send, *stages[0])]
-    came.append(exchange(part_of(keep, came, 1).astype(jnp.bfloat16), *stages[1]))
-    came.append(exchange(part_of(keep, came, 0, 1).astype(jnp.bfloat16), *stages[2]))
-    return (keep, *came)
-
-
-def join_kernel(*refs):
-    halves, outs = (refs[:4], refs[4:8]), refs[8:]
-    half = refs[0].shape[-1]
-    for n, (keep, *came) in enumerate(halves):
+def halve(kept, axis, mask):
+    half = kept[-1].shape[0] // 2
+    part = add_up([v[half : 2 * half] for v in kept]).astype(jnp.bfloat16)
+    return kept + [exchange(part, axis, mask)]
+
+
+def join_kernel(count, *refs):
+    groups, outs = (refs[:count], refs[count : 2 * count]), refs[2 * count :]
+    for n, group in enumerate(groups):
         for m, out in enumerate(outs):
-            total = part_of(keep, came, 0, 0, m)
-            out[:, n * half : (n + 1) * half] = total.astype(out.dtype)
-
-
-def join(first, second):
-    _, _, last, tall, half = first[0].shape
+            total = add_up([v[m] for v in group])
+            width = total.shape[1]
+            out[:, n * width : (n + 1) * width] = total.astype(out.dtype)
+
+
+def join(first, second, last):
+    _, tall, width = first[-1].shape
     vmem = pl.BlockSpec(memory_space=pltpu.VMEM)
     kinds = [jnp.float32] + [jnp.bfloat16] * (last - 1)
     return pl.pallas_call(
-        join_kernel,
-        out_shape=[pltpu.VMEM((tall, 2 * half), kind) for kind in kinds],
-        in_specs=[vmem] * 8,
+        functools.partial(join_kernel, len(first)),
+        out_shape=[pltpu.VMEM((tall, 2 * width), kind) for kind in kinds],
+        in_specs=[vmem] * (2 * len(first)),
         out_specs=[vmem] * last,
         compiler_params=pltpu.CompilerParams(vmem_limit_bytes=4 * 2**20),
         name="join",
@@ -465,19 +516,32 @@
     finished,
     owners,
 ):
-    steps_count, row_count, heads_here, head_size = queries.shape
+    steps_count, row_count, _, _ = queries.shape
+    replicas = lax.axis_size("replica")
     model = out_weight.shape[2]
     split = attend_split(queries, cache_keys, cache_values, new_keys, new_values, lengths)
     gathered = lax.all_to_all(split, "replica", split_axis=0, concat_axis=0, tiled=True)
     gathered = gathered.reshape(-1, gathered.shape[2])
-    weight = pltpu.with_memory_space_constraint(out_weight.reshape(-1, model), pltpu.HBM)
-    rows, base_rows, early, late = select_rows(owners, finished, weight, steps_count, row_count)
+    weight = out_weight.reshape(-1, model)
+    cols = model // replicas
+    half = cols // 2
+    calls = ((0, half), (half, half))
+    rows, base_rows, *near = select_rows(
+        owners, finished, weight, calls, EARLY, steps_count, row_count
+    )
     operands = (gathered, rows, base_rows, base_stream)
     core, across = ("tensor", 1), ("tensor", 2)
     beside, along = ("replica", 1), ("replica", 2)
-    second = first_stages(*project(1, *operands, early, weight), (core, beside, across))
-    first = first_stages(*project(0, *operands, late, weight), (core, across, beside))
-    own, *sends = join(first, second)
+    later = (calls[1], EARLY[1])
+    keep, send, rest = project(calls[0], "xyz", later, *operands, near[0], weight)
+    first = [keep, exchange(send, *core)]
+    keep, send = project(calls[1], "yxz", None, *operands, near[1], rest)
+    second = [keep, exchange(send, *core)]
+    first = halve(first, *across)
+    first = halve(first, *beside)
+    second = halve(second, *beside)
+    second = halve(second, *across)
+    own, *sends = join(first, second, replicas // 2)
     came = [exchange(v, along[0], along[1] * (m + 1)) for m, v in enumerate(sends)]
     updates, trainer_rows = finish(steps_count, (own, *came))
     return (updates, trainer_rows.reshape(1, SLOT_DEV, model))
@@ -493,7 +557,10 @@
     shares = replicas * row_count // tensors
     powers = all(n & (n - 1) == 0 for n in (replicas, steps_count, row_count, shares))
     fits = tensors == 4 and replicas == group == 8 and powers and head_size == LANES
-    return (move_sums if few and fits else regroup_weight)(*arrays)
+    fits = fits and out_weight.shape[2] % (replicas * 2 * LANES) == 0
+    if not (few and fits):
+        return regroup_weight(*arrays)
+    return move_sums(*arrays)
 
 
 def solution(mesh):

time: 51.1 us -> 50.1 us (0.980)
  Pallas kernels: 11.9 us -> 9.93 us
  waiting for transfers between devices: 21.4 us -> 22.5 us
    pallas_call x2, Pallas kernels: 5.9 us -> 4.87 us  [the longest x1 4.71 us: attend_split(): pl.pallas_call(functools.partial(attend_kernel, math.log2(math.e) / math....]
    ppermute x9, waiting for transfers between devices: 17.1 us -> 17.7 us  [exchange(): return lax.ppermute(value, axis, [(i, i ^ mask) for i in range(size)])]
    all_to_all x1, waiting for transfers between devices: 4.31 us -> 4.84 us  [move_sums(): lax.all_to_all(split, 'replica', split_axis=0, concat_axis=0, tiled=True)]
  transfers between devices with their start and end apart: 10 -> 10, of which waited for: 8 -> 8; matrix products, arithmetic and copies ran while one was open for 1% -> 1% of each run, Pallas kernels for 9% -> 4%
where the time goes in v4:
time: 50.1 us; the launch traced here: 49.9 us
  waiting for transfers between devices  22.5 us (45%)
  starting transfers between devices  16.4 us (33%)
  Pallas kernels  9.93 us (20%)
  between operations  0.71 us (1%)
    ppermute x9, waiting for transfers between devices, exchange(): return lax.ppermute(value, axis, [(i, i ^ mask) for i in range(size)])  17.7 us
    ppermute x9, starting transfers between devices, exchange(): return lax.ppermute(value, axis, [(i, i ^ mask) for i in range(size)])  9.05 us
    all_to_all x1, starting transfers between devices, move_sums(): lax.all_to_all(split, 'replica', split_axis=0, concat_axis=0, tiled=True)  7.32 us
    all_to_all x1, waiting for transfers between devices, move_sums(): lax.all_to_all(split, 'replica', split_axis=0, concat_axis=0, tiled=True)  4.84 us
    pallas_call x1, Pallas kernels, attend_split(): pl.pallas_call(functools.partial(attend_kernel, math.log2(math.e) / math....  4.71 us
    pallas_call x2, Pallas kernels, project(): pl.pallas_call(functools.partial(project_kernel, (tensors, replicas, tall...  2.34 us
    pallas_call x1, Pallas kernels, select_rows(): pl.pallas_call(functools.partial(select_kernel, (tensors, replicas, steps...  2.05 us
  transfers between devices with their start and end apart: 10, of which 8 were waited for; matrix products, arithmetic and copies ran while one was open for 1% of the time, Pallas kernels for 4%

profile of v4, /device:TPU:0, one launch (start us, length us, event | category | flops | bytes accessed | tf_op | source)
XLA Modules:
  0.0 49.9 jit_solution(4052924975631259119)
XLA Ops:
  0.6 4.7 %attend.1 = bf16[8,16,256]{2,1,0:T(8,128)(2,1)} custom-call(s32[4]{0:T(128)} %refs_0_.1, bf16[4,4,16,128]{3,2,1,0:T(8,128)(2,1)} %refs_1_.1, bf16[4,4,2,128]{3,2,1,0:T(2,128)(2,1)} %refs_2_.1, bf16[4,4,2,128]{3,2,1,0:T(2,128)(2,1)} %refs_3_.3, bf16[4,2,1536,128]{3,2,1,0:T(8,128)(2,1)} %refs_4_.1, bf16[4,2,1536,128]{3,2,1,0:T(8,128)(2,1)} %refs_5_.1), custom_call_target="tpu_custom_call" | custom-call | flops 201326592 | bytes 6291456 | tf_op jit(solution)/shard_map/attend/pallas_call | solution.py:224
  5.3 0.0 copy-start
  5.4 7.3 %all-to-all-start = ((bf16[8,16,256]{2,1,0:T(8,128)(2,1)}), bf16[8,16,256]{2,1,0:T(8,128)(2,1)S(1)}, u32[]{:S(2)}, u32[]{:S(2)}) async-start(bf16[8,16,256]{2,1,0:T(8,128)(2,1)} %attend.1), calls=%async_computation | async-start | bytes 131072 | tf_op jit(solution)/shard_map/all_to_all | solution.py:523
  12.7 2.1 %select.1 = (bf16[160,128]{1,0:T(8,128)(2,1)S(1)}, bf16[32,8]{1,0:T(8,128)(2,1)S(1)}, bf16[256,4096]{1,0:T(8,128)(2,1)S(1)}, bf16[256,2560]{1,0:T(8,128)(2,1)S(1)}) custom-call(s32[32]{0:T(128)} %bitcast.8, s32[32]{0:T(128)} %finished_at.1, bf16[256,8192]{1,0:T(8,128)(2,1)} %bitcast.6), custom_call_target="tpu_custom_call" | custom-call | flops 1000000 | bytes 4194304 | tf_op jit(solution)/shard_map/select/pallas_call | solution.py:323
  14.7 4.8 %all-to-all-done = bf16[8,16,256]{2,1,0:T(8,128)(2,1)S(1)} async-done(((bf16[8,16,256]{2,1,0:T(8,128)(2,1)}), bf16[8,16,256]{2,1,0:T(8,128)(2,1)S(1)}, u32[]{:S(2)}, u32[]{:S(2)}) %all-to-all-start) | async-done | bytes 65568 | tf_op jit(solution)/shard_map/all_to_all | solution.py:523
  19.6 0.0 copy-done
  19.6 1.7 %shard_map.113 = (bf16[16,40,512]{2,1,0:T(8,128)(2,1)S(1)}, bf16[16,40,512]{2,1,0:T(8,128)(2,1)S(1)}, bf16[256,1536]{1,0:T(8,128)(2,1)S(1)}) custom-call(bf16[128,256]{1,0:T(8,128)(2,1)S(1)} %bitcast.4, bf16[160,128]{1,0:T(8,128)(2,1)S(1)} %get-tuple-element.17.refs_1_, bf16[32,8]{1,0:T(8,128)(2,1)S(1)} %get-tuple-element.18.refs_2_, ...), custom_call_target="tpu_custom_call" | custom-call | flops 335544320 | bytes 2097152 | tf_op jit(solution)/shard_map/pallas_call | solution.py:423
  21.3 0.7 %shard_map.114 = (bf16[16,40,512]{2,1,0:T(8,128)(2,1)S(1)}, bf16[16,40,512]{2,1,0:T(8,128)(2,1)S(1)}) custom-call(bf16[128,256]{1,0:T(8,128)(2,1)S(1)} %bitcast.5, bf16[160,128]{1,0:T(8,128)(2,1)S(1)} %get-tuple-element.17.refs_1_, bf16[32,8]{1,0:T(8,128)(2,1)S(1)} %get-tuple-element.18.refs_2_, bf16[8,1024]{1,0:T(8,128)(2,1)S(1)} %copy-done, ...), custom_call_target="tpu_custom_call" | custom-call | flops 335544320 | bytes 2097152 | tf_op jit(solution)/shard_map/pallas_call | solution.py:423
  21.9 0.1 collective-permute-start.3
  22.0 0.5 collective-permute-start
  22.5 1.6 %collective-permute-done.3.refs_5_ = bf16[16,40,512]{2,1,0:T(8,128)(2,1)S(1)} collective-permute-done((bf16[16,40,512]{2,1,0:T(8,128)(2,1)S(1)}, bf16[16,40,512]{2,1,0:T(8,128)(2,1)S(1)}, u32[]{:S(2)}, u32[]{:S(2)}) %collective-permute-start.3) | collective-permute-done | bytes 655392 | tf_op jit(solution)/shard_map/ppermute | solution.py:442
  24.1 0.1 add_convert_fusion
  24.2 0.5 collective-permute-start.4
  24.7 0.4 collective-permute-done.refs_1_
  25.0 0.1 add_convert_fusion.1
  25.1 1.6 %collective-permute-start.1 = (bf16[8,40,512]{2,1,0:T(8,128)(2,1)S(1)}, bf16[8,40,512]{2,1,0:T(8,128)(2,1)S(1)}, u32[]{:S(2)}, u32[]{:S(2)}) collective-permute-start(bf16[8,40,512]{2,1,0:T(8,128)(2,1)S(1)} %add_convert_fusion.1), channel_id=1, source_target_pairs={{0,2},{1,3},{2,0},{3,1},{4,6},{5,7},{6,4},{7,5},{8,10},{9,11},{10,... | collective-permute-start | bytes 983048 | tf_op jit(solution)/shard_map/ppermute | solution.py:442
  26.7 7.3 %collective-permute-done.4.refs_6_ = bf16[8,40,512]{2,1,0:T(8,128)(2,1)S(1)} collective-permute-done((bf16[8,40,512]{2,1,0:T(8,128)(2,1)S(1)}, bf16[8,40,512]{2,1,0:T(8,128)(2,1)S(1)}, u32[]{:S(2)}, u32[]{:S(2)}) %collective-permute-start.4) | collective-permute-done | bytes 327712 | tf_op jit(solution)/shard_map/ppermute | solution.py:442
  34.0 0.1 add_convert_fusion.2
  34.1 1.6 %collective-permute-start.5 = (bf16[4,40,512]{2,1,0:T(8,128)(2,1)S(1)}, bf16[4,40,512]{2,1,0:T(8,128)(2,1)S(1)}, u32[]{:S(2)}, u32[]{:S(2)}) collective-permute-start(bf16[4,40,512]{2,1,0:T(8,128)(2,1)S(1)} %add_convert_fusion.2), channel_id=1, source_target_pairs={{0,2},{1,3},{2,0},{3,1},{4,6},{5,7},{6,4},{7,5},{8,10},{9,11},{10,... | collective-permute-start | bytes 491528 | tf_op jit(solution)/shard_map/ppermute | solution.py:442
  35.6 0.0 collective-permute-done.1.refs_2_
  35.6 0.1 add_convert_fusion.3
  35.7 0.5 collective-permute-start.2
  36.2 3.4 %collective-permute-done.5.refs_7_ = bf16[4,40,512]{2,1,0:T(8,128)(2,1)S(1)} collective-permute-done((bf16[4,40,512]{2,1,0:T(8,128)(2,1)S(1)}, bf16[4,40,512]{2,1,0:T(8,128)(2,1)S(1)}, u32[]{:S(2)}, u32[]{:S(2)}) %collective-permute-start.5) | collective-permute-done | bytes 163872 | tf_op jit(solution)/shard_map/ppermute | solution.py:442
  39.5 1.6 %collective-permute-done.2.refs_3_ = bf16[4,40,512]{2,1,0:T(8,128)(2,1)S(1)} collective-permute-done((bf16[4,40,512]{2,1,0:T(8,128)(2,1)S(1)}, bf16[4,40,512]{2,1,0:T(8,128)(2,1)S(1)}, u32[]{:S(2)}, u32[]{:S(2)}) %collective-permute-start.2) | collective-permute-done | bytes 163872 | tf_op jit(solution)/shard_map/ppermute | solution.py:442
  41.1 0.2 join.1
  41.3 0.3 collective-permute-start.6
  41.5 0.9 %collective-permute-start.7 = (bf16[40,1024]{1,0:T(8,128)(2,1)S(1)}, bf16[40,1024]{1,0:T(8,128)(2,1)S(1)}, u32[]{:S(2)}, u32[]{:S(2)}) collective-permute-start(bf16[40,1024]{1,0:T(8,128)(2,1)S(1)} %get-tuple-element.28), channel_id=1, source_target_pairs={{0,16},{4,20},{8,24},{12,28},{16,0},{20,4},{24,8},{28,12},{1,17},{... | collective-permute-start | bytes 245768 | tf_op jit(solution)/shard_map/ppermute | solution.py:442
  42.4 3.3 %collective-permute-start.8 = (bf16[40,1024]{1,0:T(8,128)(2,1)S(1)}, bf16[40,1024]{1,0:T(8,128)(2,1)S(1)}, u32[]{:S(2)}, u32[]{:S(2)}) collective-permute-start(bf16[40,1024]{1,0:T(8,128)(2,1)S(1)} %get-tuple-element.29), channel_id=1, source_target_pairs={{0,24},{4,28},{8,16},{12,20},{16,8},{20,12},{24,0},{28,4},{1,25},{... | collective-permute-start | bytes 245768 | tf_op jit(solution)/shard_map/ppermute | solution.py:442
  45.7 1.7 %collective-permute-done.6.refs_1_ = bf16[40,1024]{1,0:T(8,128)(2,1)S(1)} collective-permute-done((bf16[40,1024]{1,0:T(8,128)(2,1)S(1)}, bf16[40,1024]{1,0:T(8,128)(2,1)S(1)}, u32[]{:S(2)}, u32[]{:S(2)}) %collective-permute-start.6) | collective-permute-done | bytes 81952 | tf_op jit(solution)/shard_map/ppermute | solution.py:442
  47.4 1.7 %collective-permute-done.7.refs_2_ = bf16[40,1024]{1,0:T(8,128)(2,1)S(1)} collective-permute-done((bf16[40,1024]{1,0:T(8,128)(2,1)S(1)}, bf16[40,1024]{1,0:T(8,128)(2,1)S(1)}, u32[]{:S(2)}, u32[]{:S(2)}) %collective-permute-start.7) | collective-permute-done | bytes 81952 | tf_op jit(solution)/shard_map/ppermute | solution.py:442
  49.2 0.0 collective-permute-done.8.refs_3_
  49.2 0.7 %finish.1 = (bf16[4,8,1024]{2,1,0:T(8,128)(2,1)}, bf16[1,8192]{1,0:T(2,128)(2,1)}) custom-call(f32[40,1024]{1,0:T(8,128)S(1)} %get-tuple-element.26.refs_0_, bf16[40,1024]{1,0:T(8,128)(2,1)S(1)} %collective-permute-done.6.refs_1_, bf16[40,1024]{1,0:T(8,128)(2,1)S(1)} %collective-permute-done.7.refs_2_, bf16[40,1024]{1,0:T(8,128)(2,1)S(1)} %collective-permute-done.8.refs_3_), custom_call_target="tpu_custom_call" | custom-call | tf_op jit(solution)/shard_map/finish/pallas_call | solution.py:494
Async XLA Ops:
  5.3 14.2 %copy-start = (bf16[8,1024]{1,0:T(8,128)(2,1)S(1)}, bf16[8,1024]{1,0:T(8,128)(2,1)}, u32[]{:S(2)}) copy-start(bf16[8,1024]{1,0:T(8,128)(2,1)} %refs_3_.5) | copy-start | bytes 49156
  5.4 14.2 %all-to-all-start = ((bf16[8,16,256]{2,1,0:T(8,128)(2,1)}), bf16[8,16,256]{2,1,0:T(8,128)(2,1)S(1)}, u32[]{:S(2)}, u32[]{:S(2)}) async-start(bf16[8,16,256]{2,1,0:T(8,128)(2,1)} %attend.1), calls=%async_computation | async-start | bytes 131072 | tf_op jit(solution)/shard_map/all_to_all | solution.py:523
  21.9 2.2 %collective-permute-start.3 = (bf16[16,40,512]{2,1,0:T(8,128)(2,1)S(1)}, bf16[16,40,512]{2,1,0:T(8,128)(2,1)S(1)}, u32[]{:S(2)}, u32[]{:S(2)}) collective-permute-start(bf16[16,40,512]{2,1,0:T(8,128)(2,1)S(1)} %get-tuple-element.25), channel_id=1, source_target_pairs={{0,1},{1,0},{2,3},{3,2},{4,5},{5,4},{6,7},{7,6},{8,9},{9,8},{10,11... | collective-permute-start | bytes 1966088 | tf_op jit(solution)/shard_map/ppermute | solution.py:442
  22.0 3.0 %collective-permute-start = (bf16[16,40,512]{2,1,0:T(8,128)(2,1)S(1)}, bf16[16,40,512]{2,1,0:T(8,128)(2,1)S(1)}, u32[]{:S(2)}, u32[]{:S(2)}) collective-permute-start(bf16[16,40,512]{2,1,0:T(8,128)(2,1)S(1)} %get-tuple-element.21), channel_id=1, source_target_pairs={{0,1},{1,0},{2,3},{3,2},{4,5},{5,4},{6,7},{7,6},{8,9},{9,8},{10,11... | collective-permute-start | bytes 1966088 | tf_op jit(solution)/shard_map/ppermute | solution.py:442
  24.2 9.8 %collective-permute-start.4 = (bf16[8,40,512]{2,1,0:T(8,128)(2,1)S(1)}, bf16[8,40,512]{2,1,0:T(8,128)(2,1)S(1)}, u32[]{:S(2)}, u32[]{:S(2)}) collective-permute-start(bf16[8,40,512]{2,1,0:T(8,128)(2,1)S(1)} %add_convert_fusion), channel_id=1, source_target_pairs={{0,4},{4,0},{8,12},{12,8},{16,20},{20,16},{24,28},{28,24},{1,5},{5... | collective-permute-start | bytes 983048 | tf_op jit(solution)/shard_map/ppermute | solution.py:442
  25.1 10.5 %collective-permute-start.1 = (bf16[8,40,512]{2,1,0:T(8,128)(2,1)S(1)}, bf16[8,40,512]{2,1,0:T(8,128)(2,1)S(1)}, u32[]{:S(2)}, u32[]{:S(2)}) collective-permute-start(bf16[8,40,512]{2,1,0:T(8,128)(2,1)S(1)} %add_convert_fusion.1), channel_id=1, source_target_pairs={{0,2},{1,3},{2,0},{3,1},{4,6},{5,7},{6,4},{7,5},{8,10},{9,11},{10,... | collective-permute-start | bytes 983048 | tf_op jit(solution)/shard_map/ppermute | solution.py:442
  34.1 5.5 %collective-permute-start.5 = (bf16[4,40,512]{2,1,0:T(8,128)(2,1)S(1)}, bf16[4,40,512]{2,1,0:T(8,128)(2,1)S(1)}, u32[]{:S(2)}, u32[]{:S(2)}) collective-permute-start(bf16[4,40,512]{2,1,0:T(8,128)(2,1)S(1)} %add_convert_fusion.2), channel_id=1, source_target_pairs={{0,2},{1,3},{2,0},{3,1},{4,6},{5,7},{6,4},{7,5},{8,10},{9,11},{10,... | collective-permute-start | bytes 491528 | tf_op jit(solution)/shard_map/ppermute | solution.py:442
  35.7 5.4 %collective-permute-start.2 = (bf16[4,40,512]{2,1,0:T(8,128)(2,1)S(1)}, bf16[4,40,512]{2,1,0:T(8,128)(2,1)S(1)}, u32[]{:S(2)}, u32[]{:S(2)}) collective-permute-start(bf16[4,40,512]{2,1,0:T(8,128)(2,1)S(1)} %add_convert_fusion.3), channel_id=1, source_target_pairs={{0,4},{4,0},{8,12},{12,8},{16,20},{20,16},{24,28},{28,24},{1,5},{5... | collective-permute-start | bytes 491528 | tf_op jit(solution)/shard_map/ppermute | solution.py:442
  41.3 6.2 %collective-permute-start.6 = (bf16[40,1024]{1,0:T(8,128)(2,1)S(1)}, bf16[40,1024]{1,0:T(8,128)(2,1)S(1)}, u32[]{:S(2)}, u32[]{:S(2)}) collective-permute-start(bf16[40,1024]{1,0:T(8,128)(2,1)S(1)} %get-tuple-element.27), channel_id=1, source_target_pairs={{0,8},{4,12},{8,0},{12,4},{16,24},{20,28},{24,16},{28,20},{1,9},{5... | collective-permute-start | bytes 245768 | tf_op jit(solution)/shard_map/ppermute | solution.py:442
  41.5 7.6 %collective-permute-start.7 = (bf16[40,1024]{1,0:T(8,128)(2,1)S(1)}, bf16[40,1024]{1,0:T(8,128)(2,1)S(1)}, u32[]{:S(2)}, u32[]{:S(2)}) collective-permute-start(bf16[40,1024]{1,0:T(8,128)(2,1)S(1)} %get-tuple-element.28), channel_id=1, source_target_pairs={{0,16},{4,20},{8,24},{12,28},{16,0},{20,4},{24,8},{28,12},{1,17},{... | collective-permute-start | bytes 245768 | tf_op jit(solution)/shard_map/ppermute | solution.py:442
  42.4 6.7 %collective-permute-start.8 = (bf16[40,1024]{1,0:T(8,128)(2,1)S(1)}, bf16[40,1024]{1,0:T(8,128)(2,1)S(1)}, u32[]{:S(2)}, u32[]{:S(2)}) collective-permute-start(bf16[40,1024]{1,0:T(8,128)(2,1)S(1)} %get-tuple-element.29), channel_id=1, source_target_pairs={{0,24},{4,28},{8,16},{12,20},{16,8},{20,12},{24,0},{28,4},{1,25},{... | collective-permute-start | bytes 245768 | tf_op jit(solution)/shard_map/ppermute | solution.py:442
